TPU v7x, 8 devices: a whole 2x2x1 slice. The times are simulated.
8 devices in a mesh: dp: 1 (over z), yax: 2 (over y), xax: 4 (over x, core).
Axes of the slice: x: 2, y: 2, z: 1, core: 2. Of those that a mesh axis runs over, the one named last changes fastest.
Arguments:
- hidden: bfloat16 [256, 2048], P('dp', 'xax')
- cache_len: int32 [256], P('dp')
- k_cache: bfloat16 [256, 8192, 128], P(('dp', 'yax', 'xax'))
- v_cache: bfloat16 [256, 8192, 128], P(('dp', 'yax', 'xax'))
- g_attn: float32 [2048], P('xax')
- w_query: bfloat16 [2048, 2048], P('xax', 'yax')
- w_key: bfloat16 [2048, 128], P('xax')
- w_value: bfloat16 [2048, 128], P('xax')
- w_gate: bfloat16 [2048, 8192], P('xax', 'yax')
- w_up: bfloat16 [2048, 8192], P('xax', 'yax')
- w_out: bfloat16 [2048, 2048], P('yax', 'xax')
- w_down: bfloat16 [8192, 2048], P('yax', 'xax')
- g_final: float32 [2048], P('xax')
- embedding: bfloat16 [50304, 2048], P('yax', 'xax')
Outputs:
- output 1: bfloat16 [256, 128], P(('dp', 'yax', 'xax'))
- output 2: bfloat16 [256, 128], P(('dp', 'yax', 'xax'))
- output 3: float32 [256, 50304], P('dp', ('yax', 'xax'))
- output 4: float32 [256], P('dp')
All inputs are finite; a program needn't handle non-finite values.
Results may differ from a plain program's by a relative error of at most 0.00831507.
Values are sent between devices in bfloat16 or wider.
A program may use at most 1 GiB of HBM per device.

v0:
```python
import jax
import jax.numpy as jnp
from jax import lax
from jax.sharding import PartitionSpec as P

EPS = 1e-6
ROPE_BASE = 10000.0


def rope_angle(positions, head_dim):
    half_dim = head_dim // 2
    inv_freq = ROPE_BASE ** (-(jnp.arange(half_dim, dtype=jnp.float32) * 2.0) / head_dim)
    return positions.astype(jnp.float32)[:, None] * inv_freq[None, :]


def rotary(values_in, angles):
    half_dim = values_in.shape[-1] // 2
    cos_a = jnp.cos(angles)
    sin_a = jnp.sin(angles)
    first = values_in[..., :half_dim]
    second = values_in[..., half_dim:]
    return jnp.concatenate([first * cos_a - second * sin_a, second * cos_a + first * sin_a], axis=-1)


def sharded_norm(values_in, gain, width):
    stats = jnp.stack([jnp.sum(values_in, axis=-1), jnp.sum(values_in * values_in, axis=-1)])
    stats = lax.psum(stats, "xax")
    row_mean = stats[0] / width
    row_var = stats[1] / width - row_mean * row_mean
    return (values_in - row_mean[:, None]) * lax.rsqrt(row_var + EPS)[:, None] * gain


def attend_local(query, k_cache, v_cache, key_new, value_new, lengths):
    score_scale = query.shape[-1] ** -0.5
    scores = jnp.einsum("bhe,bse->bhs", query, k_cache, preferred_element_type=jnp.float32) * score_scale
    score_new = jnp.einsum("bhe,be->bh", query, key_new, preferred_element_type=jnp.float32) * score_scale
    valid = jnp.arange(k_cache.shape[1])[None, None, :] < lengths[:, None, None]
    row_max = jnp.maximum(jnp.max(jnp.where(valid, scores, -jnp.inf), axis=-1), score_new)
    weights = jnp.where(valid, jnp.exp(scores - row_max[..., None]), 0.0)
    weight_new = jnp.exp(score_new - row_max)
    denominator = jnp.sum(weights, axis=-1) + weight_new
    prob_all = (weights / denominator[..., None]).astype(jnp.bfloat16)
    prob_new = (weight_new / denominator).astype(jnp.bfloat16)
    attn_out = jnp.einsum("bhs,bse->bhe", prob_all, v_cache, preferred_element_type=jnp.float32)
    attn_out = attn_out + prob_new.astype(jnp.float32)[..., None] * value_new.astype(jnp.float32)[:, None, :]
    return attn_out.astype(jnp.bfloat16)


def solution(mesh):
    y_size = mesh.shape["yax"]
    x_size = mesh.shape["xax"]
    row_spec = P(("dp", "yax", "xax"))

    def local_step(hidden, cache_len, k_cache, v_cache, g_attn, w_query, w_key, w_value,
                   w_gate, w_up, w_out, w_down, g_final, embedding):
        rows = hidden.shape[0]
        width = hidden.shape[1] * x_size
        own_rows = k_cache.shape[0]
        head_dim = k_cache.shape[2]
        q_cols = w_query.shape[1]
        kv_end = q_cols + 2 * head_dim
        ff_end = kv_end + w_gate.shape[1]
        y_idx = lax.axis_index("yax")
        x_idx = lax.axis_index("xax")
        own_start = (y_idx * x_size + x_idx) * own_rows

        residual = hidden.astype(jnp.float32)
        normed = sharded_norm(residual, g_attn, width).astype(jnp.bfloat16)
        proj_part = jnp.concatenate([
            jnp.dot(normed, w_query, preferred_element_type=jnp.float32),
            jnp.dot(normed, w_key, preferred_element_type=jnp.float32),
            jnp.dot(normed, w_value, preferred_element_type=jnp.float32),
            jnp.dot(normed, w_gate, preferred_element_type=jnp.float32),
            jnp.dot(normed, w_up, preferred_element_type=jnp.float32)], axis=1)
        projected = lax.psum(proj_part, "xax").astype(jnp.bfloat16)
        angles = rope_angle(cache_len, head_dim)
        query = projected[:, :q_cols].astype(jnp.float32).reshape(rows, q_cols // head_dim, head_dim)
        query = rotary(query, angles[:, None, :]).astype(jnp.bfloat16)
        key_new = rotary(projected[:, q_cols:q_cols + head_dim].astype(jnp.float32), angles).astype(jnp.bfloat16)
        value_new = projected[:, q_cols + head_dim:kv_end]
        gate = projected[:, kv_end:ff_end]
        up_val = projected[:, ff_end:]

        query_grp = lax.all_to_all(query, "yax", 0, 1, tiled=True)
        query_own = lax.dynamic_slice_in_dim(query_grp, x_idx * own_rows, own_rows, axis=0)
        key_own = lax.dynamic_slice_in_dim(key_new, own_start, own_rows, axis=0)
        value_own = lax.dynamic_slice_in_dim(value_new, own_start, own_rows, axis=0)
        len_own = lax.dynamic_slice_in_dim(cache_len, own_start, own_rows, axis=0)
        attn_own = attend_local(query_own, k_cache, v_cache, key_own, value_own, len_own)
        attn_grp = lax.all_gather(attn_own, "xax", axis=0, tiled=True)
        attn_heads = lax.all_to_all(attn_grp, "yax", 1, 0, tiled=True).reshape(rows, q_cols)

        mlp_act = (jax.nn.silu(gate.astype(jnp.float32)) * up_val.astype(jnp.float32)).astype(jnp.bfloat16)
        branch_sum = (jnp.dot(attn_heads, w_out, preferred_element_type=jnp.float32)
                      + jnp.dot(mlp_act, w_down, preferred_element_type=jnp.float32))
        residual_out = residual + lax.psum(branch_sum, "yax")
        final_norm = sharded_norm(residual_out, g_final, width).astype(jnp.bfloat16)
        logit_part = jnp.einsum("bd,vd->bv", final_norm, embedding, preferred_element_type=jnp.float32)
        logits = lax.psum_scatter(logit_part, "xax", scatter_dimension=1, tiled=True)
        row_max = lax.pmax(jnp.max(logits, axis=1), ("yax", "xax"))
        sum_exp = lax.psum(jnp.sum(jnp.exp(logits - row_max[:, None]), axis=1), ("yax", "xax"))
        log_norm = row_max + jnp.log(sum_exp)
        return key_own, value_own, logits - log_norm[:, None], log_norm

    in_specs = (P("dp", "xax"), P("dp"), row_spec, row_spec, P("xax"), P("xax", "yax"),
                P("xax", None), P("xax", None), P("xax", "yax"), P("xax", "yax"),
                P("yax", "xax"), P("yax", "xax"), P("xax"), P("yax", "xax"))
    out_specs = (row_spec, row_spec, P("dp", ("yax", "xax")), P("dp"))
    return jax.shard_map(local_step, mesh=mesh, in_specs=in_specs, out_specs=out_specs, check_vma=False)
```

profile of v0, /device:TPU:0, one launch (start us, length us, event | category | flops | bytes accessed | tf_op | source)
XLA Modules:
  0.0 596.2 jit_solution(10131154341279583435)
XLA Ops:
  7.2 0.0 copy-start
  7.2 1.2 convert_reduce_fusion
  8.5 8.8 %psum.35 = f32[2,256]{1,0:T(2,128)S(1)} all-reduce(f32[2,256]{1,0:T(2,128)S(1)} %pad_maximum_fusion.1), channel_id=1, replica_groups=mesh['dp'=1,'yax'=2,'xax'=4] {'xax'}, use_global_device_ids=true, to_apply=%region_2.0 | all-reduce | flops 512 | bytes 4096 | tf_op jit(solution)/shard_map/psum | solution.py:27
  17.2 2.6 convolution_dynamic-update-slice_fusion.2
  19.8 2.0 convolution_dynamic-update-slice_fusion.4
  21.8 2.0 convolution_dynamic-update-slice_fusion.3
  23.8 5.6 convolution_dynamic-update-slice_fusion.1
  29.4 3.4 convolution_dynamic-update-slice_fusion
  32.8 168.2 %all-reduce.4 = bf16[256,9472]{1,0:T(8,128)(2,1)} all-reduce(f32[256,9472]{1,0:T(8,128)} %convolution_dynamic-update-slice_fusion), channel_id=1, replica_groups=mesh['dp'=1,'yax'=2,'xax'=4] {'xax'}, use_global_device_ids=true, to_apply=%region_3.0 | all-reduce | flops 2424832 | bytes 14548992 | tf_op jit(solution)/shard_map/psum | solution.py:75
  201.0 0.9 fusion.46
  201.9 1.1 convert_bitcast_fusion
  203.1 0.2 copy.34
  203.3 0.6 multiply_cosine_fusion
  203.9 0.5 subtract_convert_fusion
  204.4 1.1 pad_maximum_fusion
  205.5 3.7 all-to-all-start
  209.2 0.1 dynamic_slice.14
  209.3 0.2 iota_compare_fusion
  209.5 0.1 fusion.32
  209.6 0.6 fusion.45
  210.2 7.6 %all-to-all-done = bf16[256,8,128]{2,1,0:T(8,128)(2,1)S(1)} async-done(((bf16[256,8,128]{2,1,0:T(8,128)(2,1)}), bf16[256,8,128]{2,1,0:T(8,128)(2,1)S(1)}, u32[]{:S(2)}, u32[]{:S(2)}) %all-to-all-start) | async-done | bytes 524320 | tf_op jit(solution)/shard_map/all_to_all | solution.py:84
  217.8 0.1 copy.43
  217.9 0.2 fusion.27
  218.1 33.0 %select_reduce_fusion = (f32[32,16]{1,0:T(8,128)S(1)}, f32[32,16,8192]{2,1,0:T(8,128)}) fusion(pred[32,8192]{1,0:T(8,128)(4,1)S(1)} %iota_compare_fusion, bf16[32,8192,128]{2,1,0:T(8,128)(2,1)} %param.16, bf16[128,16,128]{2,1,0:T(8,128)(2,1)S(1)} %bitcast.42, s32[]{:T(128)S(6)} %select_n.16), kind=kOutput, calls=%fused_computation.2 | convolution fusion | flops 1086324224 | bytes 84281344 | tf_op jit(solution)/shard_map/bhe,bse->bhs/dot_general | solution.py:35
  251.1 8.4 %fusion = f32[32,16]{1,0:T(8,128)S(1)} fusion(f32[32,16,8192]{2,1,0:T(8,128)} %get-tuple-element.27, f32[32,16]{1,0:T(8,128)S(1)} %multiply_maximum_fusion, pred[32,8192]{1,0:T(8,128)(4,1)S(1)} %iota_compare_fusion), kind=kLoop, calls=%fused_computation.3 | loop fusion | flops 16776704 | bytes 17043456 | tf_op jit(solution)/shard_map/reduce_sum | solution.py:41
  259.5 28.1 %fusion.15 = bf16[32,16,128]{2,1,0:T(8,128)(2,1)S(1)} fusion(bf16[32,8192,128]{2,1,0:T(8,128)(2,1)} %param.17, f32[32,16,8192]{2,1,0:T(8,128)} %get-tuple-element.27, f32[32,16]{1,0:T(8,128)S(1)} %get-tuple-element.17, f32[32,16]{1,0:T(8,128)S(1)} %multiply_maximum_fusion, pred[32,8192]{1,0:T(8,128)(4,1)S(1)} %iota_compare_fusion, ...), kind=kOutput, calls=%fused_computation.27 | convolution fusion | flops 1094909952 | bytes 84301824 | tf_op jit(solution)/shard_map/bhs,bse->bhe/dot_general | solution.py:44
  287.6 9.7 %all_gather.3 = bf16[128,16,128]{2,1,0:T(8,128)(2,1)S(1)} all-gather(bf16[32,16,128]{2,1,0:T(8,128)(2,1)S(1)} %fusion.15), channel_id=1, replica_groups=mesh['dp'=1,'yax'=2,'xax'=4] {'xax'}, dimensions={0}, use_global_device_ids=true | all-gather | bytes 655360 | tf_op jit(solution)/shard_map/all_gather | solution.py:90
  297.3 0.9 copy.28
  298.2 3.5 all-to-all-start.1
  301.7 0.0 copy-start.6
  301.7 0.0 all-reduce.3.cloned.1.call-start
  301.8 4.9 fusion.12
  306.7 2.5 all-to-all-done.1
  309.2 0.3 copy.29
  309.6 1.2 convolution_add_fusion
  310.8 0.0 all-reduce.3.cloned.1.call-update
  310.8 0.0 reduce-scatter.2.cloned.1.call-start
  310.9 21.8 %all-reduce.3.cloned.1.call-done = f32[256,512]{1,0:T(8,128)} async-done(((f32[256,512]{1,0:T(8,128)}), f32[256,512]{1,0:T(8,128)}) %all-reduce.3.cloned.1.call-update) | async-done | bytes 524304 | tf_op jit(solution)/shard_map/psum | solution.py:96
  332.7 1.2 fusion.26
  333.9 6.5 %psum.38 = f32[2,256]{1,0:T(2,128)S(1)} all-reduce(f32[2,256]{1,0:T(2,128)S(1)} %pad_maximum_fusion.2), channel_id=1, replica_groups=mesh['dp'=1,'yax'=2,'xax'=4] {'xax'}, use_global_device_ids=true, to_apply=%region_9.10 | all-reduce | flops 512 | bytes 4096 | tf_op jit(solution)/shard_map/psum | solution.py:27
  340.4 16.8 %fusion.22 = f32[256,25152]{0,1:T(8,128)} fusion(bf16[25152,512]{1,0:T(8,128)(2,1)} %param.27, f32[512]{0:T(512)S(1)} %copy-done.6, f32[256]{0:T(256)S(1)} %add_rsqrt_fusion, f32[256]{0:T(256)S(1)} %bitcast.44, f32[256,512]{1,0:T(8,128)} %all-reduce.3.cloned.1.call-done, bf16[256,512]{1,0:T(8,128)(2,1)S(1)} %copy-done.2), kind=kOutput, calls=%fused_computation.46 | convolution fusion | flops 6594232320 | bytes 52301824 | tf_op jit(solution)/shard_map/bd,vd->bv/dot_general | solution.py:98
  357.2 0.0 reduce-scatter.2.cloned.1.call-update
  357.3 172.3 %reduce-scatter.2.cloned.1.call-done = f32[256,6288]{0,1:T(8,128)} async-done(((f32[256,25152]{0,1:T(8,128)}), f32[256,6288]{0,1:T(8,128)}) %reduce-scatter.2.cloned.1.call-update) | async-done | bytes 6438928 | tf_op jit(solution)/shard_map/reduce_scatter | solution.py:99
  529.6 3.8 reduce_max.19
  533.3 22.3 %pmax.7 = f32[256]{0:T(256)S(1)} all-reduce(f32[256]{0:T(256)S(1)} %reduce_max.19), channel_id=1, replica_groups=mesh['dp'=1,'yax'=2,'xax'=4] {'yax','xax'}, use_global_device_ids=true, to_apply=%region_12.13 | all-reduce | flops 256 | bytes 2048 | tf_op jit(solution)/shard_map/pmax | solution.py:100
  555.6 3.7 exponential_reduce_fusion
  559.4 24.0 %psum.39 = f32[256]{0:T(256)S(1)} all-reduce(f32[256]{0:T(256)S(1)} %exponential_reduce_fusion), channel_id=1, replica_groups=mesh['dp'=1,'yax'=2,'xax'=4] {'yax','xax'}, use_global_device_ids=true, to_apply=%region_14.15 | all-reduce | flops 256 | bytes 2048 | tf_op jit(solution)/shard_map/psum | solution.py:101
  583.3 6.0 %broadcast_subtract_fusion = f32[256,6288]{0,1:T(8,128)} fusion(f32[256,6288]{0,1:T(8,128)} %reduce-scatter.2.cloned.1.call-done, f32[256]{0:T(256)S(1)} %log_add_fusion), kind=kLoop, calls=%fused_computation.20 | loop fusion | flops 1609728 | bytes 12878848 | tf_op jit(solution)/shard_map/sub | solution.py:103
  (29 shorter events, 0.1 us)
Async XLA Ops:
  7.2 10.1 %copy-start = (bf16[512,1024]{1,0:T(8,128)(2,1)S(1)}, bf16[512,1024]{1,0:T(8,128)(2,1)}, u32[]{:S(2)}) copy-start(bf16[512,1024]{1,0:T(8,128)(2,1)} %param.19) | copy-start | bytes 3145732
  7.2 22.2 %copy-start.2 = (bf16[256,512]{1,0:T(8,128)(2,1)S(1)}, bf16[256,512]{1,0:T(8,128)(2,1)}, u32[]{:S(2)}) copy-start(bf16[256,512]{1,0:T(8,128)(2,1)} %param.14) | copy-start | bytes 786436
  7.2 22.2 %copy-start.5 = (f32[512]{0:T(512)S(1)}, f32[512]{0:T(512)}, u32[]{:S(2)}) copy-start(f32[512]{0:T(512)} %param.18) | copy-start | bytes 6148
  17.2 12.1 %copy-start.3 = (bf16[512,4096]{1,0:T(8,128)(2,1)S(1)}, bf16[512,4096]{1,0:T(8,128)(2,1)}, u32[]{:S(2)}) copy-start(bf16[512,4096]{1,0:T(8,128)(2,1)} %param.23) | copy-start | bytes 12582916
  32.8 170.3 %copy-start.9 = (s32[256]{0:T(256)S(1)}, s32[256]{0:T(256)}, u32[]{:S(2)}) copy-start(s32[256]{0:T(256)} %param.15) | copy-start | bytes 3076
  205.5 12.3 %all-to-all-start = ((bf16[256,8,128]{2,1,0:T(8,128)(2,1)}), bf16[256,8,128]{2,1,0:T(8,128)(2,1)S(1)}, u32[]{:S(2)}, u32[]{:S(2)}) async-start(bf16[256,8,128]{2,1,0:T(8,128)(2,1)} %pad_maximum_fusion), calls=%async_computation | async-start | bytes 1048576 | tf_op jit(solution)/shard_map/all_to_all | solution.py:84
  209.6 41.5 %copy-start.7 = (bf16[32,128]{1,0:T(8,128)(2,1)}, bf16[32,128]{1,0:T(8,128)(2,1)S(1)}, u32[]{:S(2)}) copy-start(bf16[32,128]{1,0:T(8,128)(2,1)S(1)} %fusion.32) | copy-start | bytes 24580
  298.2 11.0 %all-to-all-start.1 = ((bf16[128,16,128]{2,0,1:T(8,128)(2,1)}), bf16[128,16,128]{2,0,1:T(8,128)(2,1)S(1)}, u32[]{:S(2)}, u32[]{:S(2)}) async-start(bf16[128,16,128]{2,0,1:T(8,128)(2,1)} %copy.28), calls=%async_computation.1 | async-start | bytes 1048576 | tf_op jit(solution)/shard_map/all_to_all | solution.py:91
  301.7 7.9 %copy-start.4 = (bf16[1024,512]{1,0:T(8,128)(2,1)S(1)}, bf16[1024,512]{1,0:T(8,128)(2,1)}, u32[]{:S(2)}) copy-start(bf16[1024,512]{1,0:T(8,128)(2,1)} %param.24) | copy-start | bytes 3145732
  301.7 38.7 %copy-start.6 = (f32[512]{0:T(512)S(1)}, f32[512]{0:T(512)}, u32[]{:S(2)}) copy-start(f32[512]{0:T(512)} %param.26) | copy-start | bytes 6148
  301.7 30.9 %all-reduce.3.cloned.1.call-start = ((), (), s32[]{:S(2)}) async-start(), calls=%async_computation.3 | async-start | bytes 1048576 | tf_op jit(solution)/shard_map/psum | solution.py:96
  310.8 218.7 %reduce-scatter.2.cloned.1.call-start = ((), (), s32[]{:S(2)}) async-start(), calls=%async_computation.4 | async-start | bytes 32194560 | tf_op jit(solution)/shard_map/reduce_scatter | solution.py:99
  529.6 59.8 %copy-start.1 = (bf16[512,1024]{1,0:T(8,128)(2,1)S(1)}, bf16[512,1024]{1,0:T(8,128)(2,1)}, u32[]{:S(2)}) copy-start(bf16[512,1024]{1,0:T(8,128)(2,1)} %param.19) | copy-start | bytes 3145732
  583.3 6.0 %copy-start.8 = (f32[256]{0:T(256)}, f32[256]{0:T(256)S(1)}, u32[]{:S(2)}) copy-start(f32[256]{0:T(256)S(1)} %log_add_fusion) | copy-start | bytes 3076
Sparse Core Ops, SparseCore 0:
  311.0 21.6 all-reduce.2
  357.4 172.1 reduce-scatter.1
where the time goes:
time: 597 us; the launch traced here: 596 us
  blocking collectives  239 us (40%)
  waiting for transfers between devices  204 us (34%)
  matrix products  99.8 us (17%)
  other arithmetic  29.5 us (5%)
  between operations  14.2 us (2%)
  starting transfers between devices  7.24 us (1%)
    reduce_scatter x1, waiting for transfers between devices, local_step(): lax.psum_scatter(logit_part, 'xax', scatter_dimension=1, tiled=True)  172 us
    psum x1, blocking collectives, local_step(): projected = lax.psum(proj_part, 'xax').astype(jnp.bfloat16)  168 us
    dot_general x1, matrix products, attend_local(): jnp.einsum('bhe,bse->bhs', query, k_cache, preferred_element_type=jnp.flo...  33 us
    dot_general x1, matrix products, attend_local(): jnp.einsum('bhs,bse->bhe', prob_all, v_cache, preferred_element_type=jnp....  28.1 us
    psum x1, blocking collectives, local_step(): lax.psum(jnp.sum(jnp.exp(logits - row_max[:, None]), axis=1), ('yax', 'xa...  24 us
    pmax x1, blocking collectives, local_step(): row_max = lax.pmax(jnp.max(logits, axis=1), ('yax', 'xax'))  22.3 us
    psum x1, waiting for transfers between devices, local_step(): residual_out = residual + lax.psum(branch_sum, 'yax')  21.8 us
    dot_general x1, matrix products, local_step(): jnp.einsum('bd,vd->bv', final_norm, embedding, preferred_element_type=jnp...  16.8 us
  transfers between devices with their start and end apart: 4, of which 4 were waited for; matrix products, arithmetic and copies ran while one was open for 1% of the time, Pallas kernels for 0%

commit v1 on v0

--- a/solution.py
+++ b/solution.py
@@ -1,6 +1,10 @@
+import functools
+
 import jax
 import jax.numpy as jnp
 from jax import lax
+from jax.experimental import pallas as pl
+from jax.experimental.pallas import tpu as pltpu
 from jax.sharding import PartitionSpec as P
 
 EPS = 1e-6
@@ -44,6 +48,229 @@
     attn_out = jnp.einsum("bhs,bse->bhe", prob_all, v_cache, preferred_element_type=jnp.float32)
     attn_out = attn_out + prob_new.astype(jnp.float32)[..., None] * value_new.astype(jnp.float32)[:, None, :]
     return attn_out.astype(jnp.bfloat16)
+
+
+MESH = pl.DeviceIdType.MESH
+V_TILE = 512
+NT_DIMS = (((1,), (1,)), ((), ()))
+
+
+def positions(x_size):
+    y_idx = lax.axis_index("yax")
+    d_idx = lax.axis_index("xax")
+    core = lax.rem(d_idx, 2)
+    chip = d_idx // 2
+    return y_idx, d_idx, core, chip
+
+
+def all_barrier(y_size, x_size, y_idx, d_idx):
+    barrier = pltpu.get_barrier_semaphore()
+    for step in range(1, y_size * x_size):
+        flat = lax.rem(y_idx * x_size + d_idx + step, y_size * x_size)
+        pl.semaphore_signal(barrier, inc=1, device_id={"yax": flat // x_size, "xax": lax.rem(flat, x_size)},
+                            device_id_type=MESH)
+    pl.semaphore_wait(barrier, y_size * x_size - 1)
+
+
+def head_kernel(y_size, x_size, f_ref, emb_ref, out_ref, norm_ref, ebuf, f_peer, send, recv, out_buf,
+                stat_own, stat_all, own_sem, peer_ssem, peer_rsem, f_ssem, f_rsem, z_ssem, z_rsem,
+                stat_ssem, stat_rsem, out_sem):
+    y_idx, d_idx, core, chip = positions(x_size)
+    partner = 2 * chip + (1 - core)
+    x_nbr = 2 * (1 - chip) + core
+    n_dev = y_size * x_size
+    flat = y_idx * x_size + d_idx
+    v_quarter = recv.shape[1]
+    half_rows = recv.shape[2]
+    chunks = recv.shape[0]
+    full_tiles = v_quarter // V_TILE
+    tail = v_quarter - full_tiles * V_TILE
+    n_tiles = full_tiles + 1
+
+    def tile_span(idx):
+        return (V_TILE if idx != full_tiles else tail)
+
+    def e_own_copy(quarter, tile, size):
+        place = 2 * (1 - chip) + core if quarter == 0 else d_idx
+        start = pl.multiple_of(place * v_quarter + tile * V_TILE, 16)
+        off = pl.multiple_of(tile * V_TILE, V_TILE)
+        return pltpu.make_async_copy(emb_ref.at[pl.ds(start, size), :], ebuf.at[0, quarter, pl.ds(off, size), :],
+                                     own_sem.at[quarter, tile])
+
+    def e_peer_copy(quarter, tile, size):
+        place = 2 * (1 - chip) + (1 - core) if quarter == 0 else partner
+        start = pl.multiple_of(place * v_quarter + tile * V_TILE, 16)
+        off = pl.multiple_of(tile * V_TILE, V_TILE)
+        return pltpu.make_async_remote_copy(
+            src_ref=emb_ref.at[pl.ds(start, size), :], dst_ref=ebuf.at[1, quarter, pl.ds(off, size), :],
+            send_sem=peer_ssem.at[quarter, tile], recv_sem=peer_rsem.at[quarter, tile],
+            device_id={"xax": partner}, device_id_type=MESH)
+
+    def z_copy(chunk, tile, size):
+        off = pl.multiple_of(tile * V_TILE, V_TILE)
+        return pltpu.make_async_remote_copy(
+            src_ref=send.at[chunk, pl.ds(off, size), :], dst_ref=recv.at[chunk, pl.ds(off, size), :],
+            send_sem=z_ssem.at[chunk, tile], recv_sem=z_rsem.at[chunk, tile],
+            device_id={"xax": x_nbr}, device_id_type=MESH)
+
+    def f_copy(chunk):
+        rows = pl.ds(chunk * half_rows, half_rows)
+        return pltpu.make_async_remote_copy(
+            src_ref=f_ref.at[rows, :], dst_ref=f_peer.at[chunk], send_sem=f_ssem.at[chunk],
+            recv_sem=f_rsem.at[chunk], device_id={"xax": partner}, device_id_type=MESH)
+
+    def over_tiles(body):
+        @pl.loop(0, full_tiles)
+        def _(tile):
+            body(tile, V_TILE)
+        body(full_tiles, tail)
+
+    @pl.loop(0, full_tiles)
+    def _(tile):
+        e_own_copy(0, tile, V_TILE).start()
+    e_own_copy(0, full_tiles, tail).start()
+    all_barrier(y_size, x_size, y_idx, d_idx)
+    for chunk in range(chunks):
+        f_copy(chunk).start()
+    over_tiles(lambda tile, size: e_peer_copy(0, tile, size).start())
+    over_tiles(lambda tile, size: e_own_copy(1, tile, size).start())
+    over_tiles(lambda tile, size: e_peer_copy(1, tile, size).start())
+
+    def partial(chunk, quarter, tile, size):
+        off = pl.multiple_of(tile * V_TILE, V_TILE)
+        f_own = f_ref[pl.ds(chunk * half_rows, half_rows), :]
+        return (lax.dot_general(ebuf[0, quarter, pl.ds(off, size), :], f_own, NT_DIMS,
+                                preferred_element_type=jnp.float32)
+                + lax.dot_general(ebuf[1, quarter, pl.ds(off, size), :], f_peer[chunk], NT_DIMS,
+                                  preferred_element_type=jnp.float32))
+
+    def send_chunk(chunk):
+        def one(tile, size):
+            if chunk == 0:
+                e_own_copy(0, tile, size).wait()
+                e_peer_copy(0, tile, size).wait_recv()
+            off = pl.multiple_of(tile * V_TILE, V_TILE)
+            send[chunk, pl.ds(off, size), :] = partial(chunk, 0, tile, size)
+
+        @pl.loop(0, full_tiles)
+        def _(tile):
+            one(tile, V_TILE)
+
+            @pl.when(tile > 0)
+            def _():
+                z_copy(chunk, tile - 1, V_TILE).start()
+        one(full_tiles, tail)
+        z_copy(chunk, full_tiles - 1, V_TILE).start()
+        z_copy(chunk, full_tiles, tail).start()
+
+    for chunk in range(chunks):
+        f_copy(chunk).wait_recv()
+        send_chunk(chunk)
+
+    def take_tile(chunk, tile, size, carry):
+        run_max, run_sum = carry
+        off = pl.multiple_of(tile * V_TILE, V_TILE)
+        if chunk == 0:
+            e_own_copy(1, tile, size).wait()
+            e_peer_copy(1, tile, size).wait_recv()
+        own = partial(chunk, 1, tile, size)
+        z_copy(chunk, tile, size).wait_recv()
+        z_val = own + recv[chunk, pl.ds(off, size), :]
+        recv[chunk, pl.ds(off, size), :] = z_val
+        z_grp = z_val.reshape(size // 8, 8, half_rows)
+        new_max = jnp.maximum(run_max, jnp.max(z_grp, axis=0))
+        new_sum = run_sum * jnp.exp(run_max - new_max) + jnp.sum(jnp.exp(z_grp - new_max[None]), axis=0)
+        return new_max, new_sum
+
+    def stat_copy(chunk, step):
+        other = lax.rem(flat + step, n_dev)
+        return pltpu.make_async_remote_copy(
+            src_ref=stat_own.at[chunk], dst_ref=stat_all.at[chunk, flat], send_sem=stat_ssem.at[chunk, step],
+            recv_sem=stat_rsem.at[chunk, step],
+            device_id={"yax": other // x_size, "xax": lax.rem(other, x_size)}, device_id_type=MESH)
+
+    def out_copy(chunk):
+        return pltpu.make_async_copy(out_buf.at[chunk], out_ref.at[pl.ds(chunk * half_rows, half_rows), :],
+                                     out_sem.at[chunk])
+
+    def finish_chunk(chunk):
+        low = jnp.full((8, half_rows), -jnp.inf, jnp.float32)
+        carry = take_tile(chunk, 0, V_TILE, (low, jnp.zeros((8, half_rows), jnp.float32)))
+        carry = lax.fori_loop(1, full_tiles, lambda tile, c: take_tile(chunk, tile, V_TILE, c), carry)
+        run_max, run_sum = take_tile(chunk, full_tiles, tail, carry)
+        top = jnp.max(run_max, axis=0, keepdims=True)
+        total = jnp.sum(run_sum * jnp.exp(run_max - top), axis=0, keepdims=True)
+        sub = lax.broadcasted_iota(jnp.int32, (8, half_rows), 0)
+        both = jnp.where(sub == 0, top, total)
+        stat_own[chunk] = both
+        stat_all[chunk, flat] = both
+        for step in range(1, n_dev):
+            stat_copy(chunk, step).start()
+        for step in range(1, n_dev):
+            stat_copy(chunk, step).wait_recv()
+        tops = [stat_all[chunk, i, 0:1, :] for i in range(n_dev)]
+        top_all = tops[0]
+        for item in tops[1:]:
+            top_all = jnp.maximum(top_all, item)
+        sum_all = jnp.zeros_like(top_all)
+        for i in range(n_dev):
+            sum_all = sum_all + stat_all[chunk, i, 1:2, :] * jnp.exp(tops[i] - top_all)
+        log_norm = top_all + jnp.log(sum_all)
+        norm_ref[:, pl.ds(chunk * half_rows, half_rows)] = log_norm
+
+        lanes = v_quarter // 128
+
+        @pl.loop(0, lanes)
+        def _(blk):
+            off = pl.multiple_of(blk * 128, 128)
+            out_buf[chunk, :, pl.ds(off, 128)] = jnp.transpose(recv[chunk, pl.ds(off, 128), :] - log_norm)
+        left = v_quarter - lanes * 128
+        if left:
+            out_buf[chunk, :, pl.ds(lanes * 128, left)] = jnp.transpose(
+                recv[chunk, pl.ds(lanes * 128, left), :] - log_norm)
+        out_copy(chunk).start()
+
+    for chunk in range(chunks):
+        finish_chunk(chunk)
+
+    for chunk in range(chunks):
+        out_copy(chunk).wait()
+        f_copy(chunk).wait_send()
+        over_tiles(lambda tile, size: z_copy(chunk, tile, size).wait_send())
+        over_tiles(lambda tile, size: e_peer_copy(chunk, tile, size).wait_send())
+        for step in range(1, n_dev):
+            stat_copy(chunk, step).wait_send()
+
+
+def head_call(mesh, final_norm, embedding):
+    y_size, x_size = mesh.shape["yax"], mesh.shape["xax"]
+    rows, width = final_norm.shape
+    v_quarter = embedding.shape[0] // x_size
+    half = rows // 2
+    tiles = v_quarter // V_TILE + 1
+    n_dev = y_size * x_size
+    dma = pltpu.SemaphoreType.DMA
+    vm = pltpu.VMEM
+    any_spec = pl.BlockSpec(memory_space=pl.ANY)
+    vmem_spec = pl.BlockSpec(memory_space=pltpu.VMEM)
+    return pl.pallas_call(
+        functools.partial(head_kernel, y_size, x_size),
+        out_shape=(jax.ShapeDtypeStruct((rows, v_quarter), jnp.float32),
+                   jax.ShapeDtypeStruct((1, rows), jnp.float32)),
+        in_specs=[vmem_spec, any_spec],
+        out_specs=(any_spec, vmem_spec),
+        scratch_shapes=[
+            vm((2, 2, v_quarter, width), jnp.bfloat16), vm((2, half, width), jnp.bfloat16),
+            vm((2, v_quarter, half), jnp.float32), vm((2, v_quarter, half), jnp.float32),
+            vm((2, half, v_quarter), jnp.float32),
+            vm((2, 8, half), jnp.float32), vm((2, n_dev, 8, half), jnp.float32),
+            dma((2, tiles)), dma((2, tiles)), dma((2, tiles)), dma((2,)), dma((2,)), dma((2, tiles)), dma((2, tiles)),
+            dma((2, n_dev)), dma((2, n_dev)), dma((2,))],
+        compiler_params=pltpu.CompilerParams(collective_id=0, has_side_effects=True, vmem_limit_bytes=62 * 1024 * 1024),
+        cost_estimate=pl.CostEstimate(flops=2 * rows * 2 * v_quarter * 2 * width, bytes_accessed=40_000_000,
+                                      transcendentals=rows * v_quarter),
+        name="head",
+    )(final_norm, embedding)
 
 
 def solution(mesh):
@@ -95,12 +322,8 @@
                       + jnp.dot(mlp_act, w_down, preferred_element_type=jnp.float32))
         residual_out = residual + lax.psum(branch_sum, "yax")
         final_norm = sharded_norm(residual_out, g_final, width).astype(jnp.bfloat16)
-        logit_part = jnp.einsum("bd,vd->bv", final_norm, embedding, preferred_element_type=jnp.float32)
-        logits = lax.psum_scatter(logit_part, "xax", scatter_dimension=1, tiled=True)
-        row_max = lax.pmax(jnp.max(logits, axis=1), ("yax", "xax"))
-        sum_exp = lax.psum(jnp.sum(jnp.exp(logits - row_max[:, None]), axis=1), ("yax", "xax"))
-        log_norm = row_max + jnp.log(sum_exp)
-        return key_own, value_own, logits - log_norm[:, None], log_norm
+        log_probs, log_norm = head_call(mesh, final_norm, embedding)
+        return key_own, value_own, log_probs, log_norm.reshape(rows)
 
     in_specs = (P("dp", "xax"), P("dp"), row_spec, row_spec, P("xax"), P("xax", "yax"),
                 P("xax", None), P("xax", None), P("xax", "yax"), P("xax", "yax"),

time: 597 us -> 529 us (0.89)
  waiting for transfers between devices: 204 us -> 32 us
  Pallas kernels: 0 us -> 170 us
  blocking collectives: 239 us -> 193 us
  matrix products: 99.8 us -> 83 us
  other arithmetic: 29.5 us -> 17.9 us
  local copies, waits for them, and re-layouts: 1.69 us -> 10.3 us
    reduce_scatter x1 -> x0, waiting for transfers between devices: 172 us -> none  [local_step(): lax.psum_scatter(logit_part, 'xax', scatter_dimension=1, tiled=True)]
    pallas_call x0 -> x1, Pallas kernels: none -> 170 us  [head_call(): pl.pallas_call(functools.partial(head_kernel, y_size, x_size), out_shape=...]
    psum x1 -> x0, blocking collectives: 24 us -> none  [local_step(): lax.psum(jnp.sum(jnp.exp(logits - row_max[:, None]), axis=1), ('yax', 'xa...]
    pmax x1 -> x0, blocking collectives: 22.3 us -> none  [local_step(): row_max = lax.pmax(jnp.max(logits, axis=1), ('yax', 'xax'))]
    dot_general x1 -> x0, matrix products: 16.8 us -> none  [local_step(): jnp.einsum('bd,vd->bv', final_norm, embedding, preferred_element_type=jnp...]
    unnamed x21 -> x23, local copies, waits for them, and re-layouts: 0.25 us -> 8.91 us
    sub x1 -> x0, other arithmetic: 6 us -> none  [local_step(): return (key_own, value_own, logits - log_norm[:, None], log_norm)]
  transfers between devices with their start and end apart: 4 -> 3, of which waited for: 4 -> 3; matrix products, arithmetic and copies ran while one was open for 1% -> 1% of each run, Pallas kernels for 0% -> 0%
where the time goes in v1:
time: 529 us; the launch traced here: 528 us
  blocking collectives  193 us (36%)
  Pallas kernels  170 us (32%)
  matrix products  83 us (16%)
  waiting for transfers between devices  32 us (6%)
  other arithmetic  17.9 us (3%)
  between operations  14.2 us (3%)
  local copies, waits for them, and re-layouts  10.3 us (2%)
  starting transfers between devices  7.2 us (1%)
    pallas_call x1, Pallas kernels, head_call(): pl.pallas_call(functools.partial(head_kernel, y_size, x_size), out_shape=...  170 us
    psum x1, blocking collectives, local_step(): projected = lax.psum(proj_part, 'xax').astype(jnp.bfloat16)  168 us
    dot_general x1, matrix products, attend_local(): jnp.einsum('bhe,bse->bhs', query, k_cache, preferred_element_type=jnp.flo...  33 us
    dot_general x1, matrix products, attend_local(): jnp.einsum('bhs,bse->bhe', prob_all, v_cache, preferred_element_type=jnp....  28.1 us
    psum x1, waiting for transfers between devices, local_step(): residual_out = residual + lax.psum(branch_sum, 'yax')  21.8 us
    psum x2, blocking collectives, sharded_norm(): stats = lax.psum(stats, 'xax')  15.3 us
  transfers between devices with their start and end apart: 3, of which 3 were waited for; matrix products, arithmetic and copies ran while one was open for 1% of the time, Pallas kernels for 0%

profile of v1, /device:TPU:0, one launch (start us, length us, event | category | flops | bytes accessed | tf_op | source)
XLA Modules:
  0.0 527.8 jit_solution(14411674768012365332)
XLA Ops:
  7.2 0.0 copy-start
  7.2 0.0 copy-start.2
  7.2 0.0 copy-start.5
  7.2 1.2 convert_reduce_fusion
  8.5 8.8 %psum.28 = f32[2,256]{1,0:T(2,128)S(1)} all-reduce(f32[2,256]{1,0:T(2,128)S(1)} %pad_maximum_fusion.1), channel_id=1, replica_groups=mesh['dp'=1,'yax'=2,'xax'=4] {'xax'}, use_global_device_ids=true, to_apply=%region_2.0 | all-reduce | flops 512 | bytes 4096 | tf_op jit(solution)/shard_map/psum | solution.py:31
  17.2 2.6 convolution_dynamic-update-slice_fusion.2
  19.8 2.0 convolution_dynamic-update-slice_fusion.4
  21.8 2.0 convolution_dynamic-update-slice_fusion.3
  23.8 5.6 %convolution_dynamic-update-slice_fusion.1 = f32[256,9472]{1,0:T(8,128)} fusion(f32[256,9472]{1,0:T(8,128)} %convolution_dynamic-update-slice_fusion.3, bf16[512,4096]{1,0:T(8,128)(2,1)} %param.22, bf16[256,512]{1,0:T(8,128)(2,1)} %param.14, f32[512]{0:T(512)} %param.18, f32[256]{0:T(256)S(1)} %add_rsqrt_fusion.1, f32[256]{0:T(256)S(1)} %bitcast.47), kind=kOutput, calls=%fused_computation.11 | convolution fusion | flops 1074397184 | bytes 8654848 | tf_op jit(solution)/shard_map/dot_general | solution.py:300
  29.3 0.0 copy-done.5
  29.4 3.4 convolution_dynamic-update-slice_fusion
  32.8 168.2 %all-reduce.4 = bf16[256,9472]{1,0:T(8,128)(2,1)} all-reduce(f32[256,9472]{1,0:T(8,128)} %convolution_dynamic-update-slice_fusion), channel_id=1, replica_groups=mesh['dp'=1,'yax'=2,'xax'=4] {'xax'}, use_global_device_ids=true, to_apply=%region_3.0 | all-reduce | flops 2424832 | bytes 14548992 | tf_op jit(solution)/shard_map/psum | solution.py:302
  201.0 0.9 fusion.42
  201.9 1.1 convert_bitcast_fusion
  203.1 0.2 copy.37
  203.3 0.6 multiply_cosine_fusion
  203.9 0.5 subtract_convert_fusion
  204.4 1.1 pad_maximum_fusion
  205.5 3.7 all-to-all-start
  209.2 0.1 dynamic_slice.14
  209.3 0.2 iota_compare_fusion
  209.5 0.1 fusion.28
  209.6 0.6 fusion.41
  210.2 7.6 %all-to-all-done = bf16[256,8,128]{2,1,0:T(8,128)(2,1)S(1)} async-done(((bf16[256,8,128]{2,1,0:T(8,128)(2,1)}), bf16[256,8,128]{2,1,0:T(8,128)(2,1)S(1)}, u32[]{:S(2)}, u32[]{:S(2)}) %all-to-all-start) | async-done | bytes 524320 | tf_op jit(solution)/shard_map/all_to_all | solution.py:311
  217.8 0.1 copy.46
  217.9 0.2 fusion.23
  218.1 33.0 %select_reduce_fusion = (f32[32,16]{1,0:T(8,128)S(1)}, f32[32,16,8192]{2,1,0:T(8,128)}) fusion(pred[32,8192]{1,0:T(8,128)(4,1)S(1)} %iota_compare_fusion, bf16[32,8192,128]{2,1,0:T(8,128)(2,1)} %param.16, bf16[128,16,128]{2,1,0:T(8,128)(2,1)S(1)} %bitcast.42, s32[]{:T(128)S(6)} %select_n.16), kind=kOutput, calls=%fused_computation.2 | convolution fusion | flops 1086324224 | bytes 84281344 | tf_op jit(solution)/shard_map/bhe,bse->bhs/dot_general | solution.py:39
  251.1 0.0 copy-done.6
  251.1 8.4 %fusion = f32[32,16]{1,0:T(8,128)S(1)} fusion(f32[32,16,8192]{2,1,0:T(8,128)} %get-tuple-element.43, f32[32,16]{1,0:T(8,128)S(1)} %multiply_maximum_fusion, pred[32,8192]{1,0:T(8,128)(4,1)S(1)} %iota_compare_fusion), kind=kLoop, calls=%fused_computation.3 | loop fusion | flops 16776704 | bytes 17043456 | tf_op jit(solution)/shard_map/reduce_sum | solution.py:45
  259.5 28.1 %fusion.15 = bf16[32,16,128]{2,1,0:T(8,128)(2,1)S(1)} fusion(bf16[32,8192,128]{2,1,0:T(8,128)(2,1)} %param.17, f32[32,16,8192]{2,1,0:T(8,128)} %get-tuple-element.43, f32[32,16]{1,0:T(8,128)S(1)} %get-tuple-element.33, f32[32,16]{1,0:T(8,128)S(1)} %multiply_maximum_fusion, pred[32,8192]{1,0:T(8,128)(4,1)S(1)} %iota_compare_fusion, ...), kind=kOutput, calls=%fused_computation.25 | convolution fusion | flops 1094909952 | bytes 84301824 | tf_op jit(solution)/shard_map/bhs,bse->bhe/dot_general | solution.py:48
  287.6 9.7 %all_gather.3 = bf16[128,16,128]{2,1,0:T(8,128)(2,1)S(1)} all-gather(bf16[32,16,128]{2,1,0:T(8,128)(2,1)S(1)} %fusion.15), channel_id=1, replica_groups=mesh['dp'=1,'yax'=2,'xax'=4] {'xax'}, dimensions={0}, use_global_device_ids=true | all-gather | bytes 655360 | tf_op jit(solution)/shard_map/all_gather | solution.py:317
  297.3 0.9 copy.30
  298.2 3.5 all-to-all-start.1
  301.7 0.0 copy-start.4
  301.7 0.0 copy-start.7
  301.7 0.0 all-reduce.3.cloned.1.call-start
  301.8 4.9 fusion.12
  306.7 2.5 all-to-all-done.1
  309.2 0.3 copy.31
  309.6 1.2 convolution_add_fusion
  310.8 0.0 all-reduce.3.cloned.1.call-update
  310.8 21.8 %all-reduce.3.cloned.1.call-done = f32[256,512]{1,0:T(8,128)} async-done(((f32[256,512]{1,0:T(8,128)}), f32[256,512]{1,0:T(8,128)}) %all-reduce.3.cloned.1.call-update) | async-done | bytes 524304 | tf_op jit(solution)/shard_map/psum | solution.py:323
  332.7 1.2 fusion.22
  333.9 6.5 %psum.31 = f32[2,256]{1,0:T(2,128)S(1)} all-reduce(f32[2,256]{1,0:T(2,128)S(1)} %pad_maximum_fusion.2), channel_id=1, replica_groups=mesh['dp'=1,'yax'=2,'xax'=4] {'xax'}, use_global_device_ids=true, to_apply=%region_9.10 | all-reduce | flops 512 | bytes 4096 | tf_op jit(solution)/shard_map/psum | solution.py:31
  340.4 1.9 multiply_convert_fusion.f_ref
  342.3 170.0 %head.1 = (f32[256,6288]{1,0:T(8,128)}, f32[1,256]{1,0:T(1,128)}) custom-call(bf16[256,512]{1,0:T(8,128)(2,1)} %multiply_convert_fusion.f_ref, bf16[25152,512]{1,0:T(8,128)(2,1)} %emb_ref.1), custom_call_target="tpu_custom_call" | custom-call | flops 6593445888 | bytes 40000000 | tf_op jit(solution)/shard_map/head/pallas_call | solution.py:256
  512.3 8.1 %copy.32 = f32[256,6288]{0,1:T(8,128)} copy(f32[256,6288]{1,0:T(8,128)} %get-tuple-element.18) | data formatting | bytes 12877824
  520.4 0.6 copy.55
  (23 shorter events, 0.1 us)
Async XLA Ops:
  7.2 10.1 %copy-start = (bf16[512,1024]{1,0:T(8,128)(2,1)S(1)}, bf16[512,1024]{1,0:T(8,128)(2,1)}, u32[]{:S(2)}) copy-start(bf16[512,1024]{1,0:T(8,128)(2,1)} %param.19) | copy-start | bytes 3145732
  7.2 22.2 %copy-start.2 = (bf16[256,512]{1,0:T(8,128)(2,1)S(1)}, bf16[256,512]{1,0:T(8,128)(2,1)}, u32[]{:S(2)}) copy-start(bf16[256,512]{1,0:T(8,128)(2,1)} %param.14) | copy-start | bytes 786436
  7.2 22.2 %copy-start.5 = (f32[512]{0:T(512)S(1)}, f32[512]{0:T(512)}, u32[]{:S(2)}) copy-start(f32[512]{0:T(512)} %param.18) | copy-start | bytes 6148
  17.2 12.1 %copy-start.3 = (bf16[512,4096]{1,0:T(8,128)(2,1)S(1)}, bf16[512,4096]{1,0:T(8,128)(2,1)}, u32[]{:S(2)}) copy-start(bf16[512,4096]{1,0:T(8,128)(2,1)} %param.23) | copy-start | bytes 12582916
  32.8 170.3 %copy-start.8 = (s32[256]{0:T(256)S(1)}, s32[256]{0:T(256)}, u32[]{:S(2)}) copy-start(s32[256]{0:T(256)} %param.15) | copy-start | bytes 3076
  205.5 12.3 %all-to-all-start = ((bf16[256,8,128]{2,1,0:T(8,128)(2,1)}), bf16[256,8,128]{2,1,0:T(8,128)(2,1)S(1)}, u32[]{:S(2)}, u32[]{:S(2)}) async-start(bf16[256,8,128]{2,1,0:T(8,128)(2,1)} %pad_maximum_fusion), calls=%async_computation | async-start | bytes 1048576 | tf_op jit(solution)/shard_map/all_to_all | solution.py:311
  209.6 41.5 %copy-start.6 = (bf16[32,128]{1,0:T(8,128)(2,1)}, bf16[32,128]{1,0:T(8,128)(2,1)S(1)}, u32[]{:S(2)}) copy-start(bf16[32,128]{1,0:T(8,128)(2,1)S(1)} %fusion.28) | copy-start | bytes 24580
  298.2 11.0 %all-to-all-start.1 = ((bf16[128,16,128]{2,0,1:T(8,128)(2,1)}), bf16[128,16,128]{2,0,1:T(8,128)(2,1)S(1)}, u32[]{:S(2)}, u32[]{:S(2)}) async-start(bf16[128,16,128]{2,0,1:T(8,128)(2,1)} %copy.30), calls=%async_computation.1 | async-start | bytes 1048576 | tf_op jit(solution)/shard_map/all_to_all | solution.py:318
  301.7 7.9 %copy-start.4 = (bf16[1024,512]{1,0:T(8,128)(2,1)S(1)}, bf16[1024,512]{1,0:T(8,128)(2,1)}, u32[]{:S(2)}) copy-start(bf16[1024,512]{1,0:T(8,128)(2,1)} %param.24) | copy-start | bytes 3145732
  301.7 38.7 %copy-start.7 = (f32[512]{0:T(512)S(1)}, f32[512]{0:T(512)}, u32[]{:S(2)}) copy-start(f32[512]{0:T(512)} %param.26) | copy-start | bytes 6148
  301.7 30.9 %all-reduce.3.cloned.1.call-start = ((), (), s32[]{:S(2)}) async-start(), calls=%async_computation.2 | async-start | bytes 1048576 | tf_op jit(solution)/shard_map/psum | solution.py:323
  342.3 178.7 %copy-start.1 = (bf16[512,1024]{1,0:T(8,128)(2,1)S(1)}, bf16[512,1024]{1,0:T(8,128)(2,1)}, u32[]{:S(2)}) copy-start(bf16[512,1024]{1,0:T(8,128)(2,1)} %param.19) | copy-start | bytes 3145732
  512.3 8.1 %copy-start.9 = (f32[1,256]{1,0:T(1,128)S(1)}, f32[1,256]{1,0:T(1,128)}, u32[]{:S(2)}) copy-start(f32[1,256]{1,0:T(1,128)} %get-tuple-element.7) | copy-start | bytes 3076
Sparse Core Ops, SparseCore 0:
  311.0 21.6 all-reduce.2

commit v2 on v1

v2 whole, which is shorter than its diff:
```python
import functools

import jax
import jax.numpy as jnp
from jax import lax
from jax.experimental import pallas as pl
from jax.experimental.pallas import tpu as pltpu
from jax.sharding import PartitionSpec as P

EPS = 1e-6
ROPE_BASE = 10000.0


def rope_angle(positions, head_dim):
    half_dim = head_dim // 2
    inv_freq = ROPE_BASE ** (-(jnp.arange(half_dim, dtype=jnp.float32) * 2.0) / head_dim)
    return positions.astype(jnp.float32)[:, None] * inv_freq[None, :]


MESH = pl.DeviceIdType.MESH
V_TILE = 512
NT_DIMS = (((1,), (1,)), ((), ()))


def positions(x_size):
    y_idx = lax.axis_index("yax")
    d_idx = lax.axis_index("xax")
    core = lax.rem(d_idx, 2)
    chip = d_idx // 2
    return y_idx, d_idx, core, chip


def all_barrier(y_size, x_size, y_idx, d_idx):
    barrier = pltpu.get_barrier_semaphore()
    for step in range(1, y_size * x_size):
        flat = lax.rem(y_idx * x_size + d_idx + step, y_size * x_size)
        pl.semaphore_signal(barrier, inc=1, device_id={"yax": flat // x_size, "xax": lax.rem(flat, x_size)},
                            device_id_type=MESH)
    pl.semaphore_wait(barrier, y_size * x_size - 1)


def compact_rows(first, second):
    rows = first.shape[0]
    lane = lax.broadcasted_iota(jnp.int32, (rows, 128), 1)
    return jnp.transpose(jnp.where(lane == 0, first, second))[0:8, :]


def spread_rows(first, second):
    rows = first.shape[1]
    sub = lax.broadcasted_iota(jnp.int32, (128, rows), 0)
    cols = jnp.transpose(jnp.where(sub == 0, first, second))
    return cols[:, 0:1], cols[:, 1:2]


def local_moments(values_in):
    part = values_in.shape[1]
    mean = jnp.sum(values_in, axis=1, keepdims=True) / part
    diff = values_in - mean
    return mean, jnp.sum(diff * diff, axis=1, keepdims=True)


def join_moments(stats, count, part):
    mean = stats[0][0:1, :]
    for item in stats[1:]:
        mean = mean + item[0:1, :]
    mean = mean / count
    square = jnp.zeros_like(mean)
    for item in stats:
        shift = item[0:1, :] - mean
        square = square + item[1:2, :] + part * shift * shift
    return mean, lax.rsqrt(square / (count * part) + EPS)


def project_kernel(y_size, x_size, hid_ref, gain_ref, cos_ref, sin_ref, wq_ref, wk_ref, wv_ref, wg_ref, wu_ref,
                   q_out, k_out, v_out, keep_out, send_a_out, send_b_out,
                   hid_peer, gain_peer, wq_buf, wkv_buf, wgu_buf, n_buf, stat_own, stat_all,
                   q_send, q_recv, kv_send, kv_recv, q_bf, q_peer, gu_buf,
                   hid_sem, stat_ssem, stat_rsem, wl_sem, wp_ssem, wp_rsem, q_sem, y_sem, out_sem):
    y_idx, d_idx, core, chip = positions(x_size)
    partner = 2 * chip + (1 - core)
    x_nbr = 2 * (1 - chip) + core
    rows, part = hid_ref.shape
    half = rows // 2
    own_rows = q_out.shape[0]
    q_cols = wq_ref.shape[1]
    head_dim = wk_ref.shape[1]
    ff_cols = wgu_buf.shape[3] // 2
    n_blk = rows // own_rows

    def ff_block(j, which_core):
        place = (2 * (1 - chip) if j == 0 else 2 * chip) + which_core
        return pl.ds(pl.multiple_of(place * ff_cols, 128), ff_cols)

    def small_dsts(side):
        return (wq_buf.at[side], wkv_buf.at[side, :, pl.ds(0, head_dim)], wkv_buf.at[side, :, pl.ds(head_dim, head_dim)])

    local = [pltpu.make_async_copy(src, dst, wl_sem.at[i])
             for i, (src, dst) in enumerate(zip((wq_ref, wk_ref, wv_ref), small_dsts(0)))]
    remote = [pltpu.make_async_remote_copy(src_ref=src, dst_ref=dst, send_sem=wp_ssem.at[i], recv_sem=wp_rsem.at[i],
                                           device_id={"xax": partner}, device_id_type=MESH)
              for i, (src, dst) in enumerate(zip((wq_ref, wk_ref, wv_ref), small_dsts(1)))]
    local_gu, remote_gu = [], []
    for j in range(2):
        for which, src in enumerate((wg_ref, wu_ref)):
            i = 3 + 2 * j + which
            dst_cols = pl.ds(which * ff_cols, ff_cols)
            local_gu.append(pltpu.make_async_copy(src.at[:, ff_block(j, core)], wgu_buf.at[0, j, :, dst_cols],
                                                  wl_sem.at[i]))
            remote_gu.append(pltpu.make_async_remote_copy(
                src_ref=src.at[:, ff_block(j, 1 - core)], dst_ref=wgu_buf.at[1, j, :, dst_cols],
                send_sem=wp_ssem.at[i], recv_sem=wp_rsem.at[i], device_id={"xax": partner}, device_id_type=MESH))
    hid_copy = pltpu.make_async_remote_copy(src_ref=hid_ref, dst_ref=hid_peer, send_sem=hid_sem.at[0],
                                            recv_sem=hid_sem.at[1], device_id={"xax": partner}, device_id_type=MESH)
    gain_copy = pltpu.make_async_remote_copy(src_ref=gain_ref, dst_ref=gain_peer, send_sem=hid_sem.at[2],
                                             recv_sem=hid_sem.at[3], device_id={"xax": partner}, device_id_type=MESH)

    def stat_copy(step):
        return pltpu.make_async_remote_copy(
            src_ref=stat_own, dst_ref=stat_all.at[d_idx], send_sem=stat_ssem.at[step], recv_sem=stat_rsem.at[step],
            device_id={"xax": lax.rem(d_idx + step, x_size)}, device_id_type=MESH)

    for item in local:
        item.start()
    all_barrier(y_size, x_size, y_idx, d_idx)
    hid_copy.start()
    gain_copy.start()
    for item in remote:
        item.start()
    for item in local_gu:
        item.start()

    hid = hid_ref[...].astype(jnp.float32)
    mean_own, square_own = local_moments(hid)
    packed = compact_rows(mean_own, square_own)
    stat_own[...] = packed
    stat_all[d_idx] = packed
    for step in range(1, x_size):
        stat_copy(step).start()
    for item in remote_gu:
        item.start()
    hid_copy.wait_recv()
    gain_copy.wait_recv()
    for step in range(1, x_size):
        stat_copy(step).wait_recv()
    mean, rstd = spread_rows(*join_moments([stat_all[i] for i in range(x_size)], x_size, part))
    n_buf[0] = ((hid - mean) * rstd * gain_ref[0:1, :]).astype(jnp.bfloat16)
    n_buf[1] = ((hid_peer[...].astype(jnp.float32) - mean) * rstd * gain_peer[0:1, :]).astype(jnp.bfloat16)

    def dest_rows(y_at, chip_at):
        return pl.ds(pl.multiple_of(y_at * half + (2 * chip_at + core) * own_rows, own_rows), own_rows)

    def two_dots(row_sets, weights):
        left = [jnp.concatenate([n_buf[side, r, :] for r in row_sets], axis=0) if len(row_sets) > 1
                else n_buf[side, row_sets[0], :] for side in range(2)]
        return (jnp.dot(left[0], weights.at[0][...], preferred_element_type=jnp.float32)
                + jnp.dot(left[1], weights.at[1][...], preferred_element_type=jnp.float32))

    for item in local:
        item.wait()
    for item in remote:
        item.wait_recv()
    q_send[...] = two_dots([dest_rows(0, 1 - chip), dest_rows(1, 1 - chip)], wq_buf)
    kv_send[...] = two_dots([dest_rows(y_idx, 1 - chip)], wkv_buf)
    q_copy = pltpu.make_async_remote_copy(src_ref=q_send, dst_ref=q_recv, send_sem=q_sem.at[0], recv_sem=q_sem.at[1],
                                          device_id={"xax": x_nbr}, device_id_type=MESH)
    kv_copy = pltpu.make_async_remote_copy(src_ref=kv_send, dst_ref=kv_recv, send_sem=q_sem.at[2],
                                           recv_sem=q_sem.at[3], device_id={"xax": x_nbr}, device_id_type=MESH)
    q_copy.start()
    q_keep = two_dots([dest_rows(0, chip), dest_rows(1, chip)], wq_buf)
    kv_copy.start()
    kv_keep = two_dots([dest_rows(y_idx, chip)], wkv_buf)

    for item in local_gu:
        item.wait()
    for item in remote_gu:
        item.wait_recv()

    gu_outs = [[pltpu.make_async_copy(gu_buf.at[0, 0], send_a_out, out_sem.at[0]),
                pltpu.make_async_copy(gu_buf.at[0, 1], send_b_out, out_sem.at[1])],
               [pltpu.make_async_copy(gu_buf.at[1, r], keep_out.at[pl.ds(r * half, half), :], out_sem.at[2 + r])
                for r in range(2)]]

    def gu_part(j, r):
        span = pl.ds(r * half, half)

        @pl.loop(0, 2 * ff_cols // 512)
        def _(t):
            cols = pl.ds(pl.multiple_of(t * 512, 512), 512)
            gu_buf[j, r, :, cols] = (
                jnp.dot(n_buf[0, span, :], wgu_buf[0, j, :, cols], preferred_element_type=jnp.float32)
                + jnp.dot(n_buf[1, span, :], wgu_buf[1, j, :, cols], preferred_element_type=jnp.float32))

    for r in range(2):
        gu_part(0, r)
        gu_outs[0][r].start()

    def rotate(values_in):
        val = values_in.astype(jnp.float32)
        return (val * cos_ref[...] + pltpu.roll(val, head_dim // 2, 1) * sin_ref[...]).astype(jnp.bfloat16)

    q_copy.wait_recv()
    q_bf[...] = (q_keep + q_recv[...]).astype(jnp.bfloat16)
    y_copy = pltpu.make_async_remote_copy(
        src_ref=q_bf.at[pl.ds(pl.multiple_of((1 - y_idx) * own_rows, own_rows), own_rows), :], dst_ref=q_peer,
        send_sem=y_sem.at[0], recv_sem=y_sem.at[1], device_id={"yax": 1 - y_idx}, device_id_type=MESH)
    y_copy.start()
    kv_copy.wait_recv()
    kv_bf = (kv_keep + kv_recv[...]).astype(jnp.bfloat16)
    k_out[...] = rotate(kv_bf[:, :head_dim])
    v_out[...] = kv_bf[:, head_dim:]
    for r in range(2):
        gu_part(1, r)
        gu_outs[1][r].start()
    own_span = pl.ds(pl.multiple_of(y_idx * own_rows, own_rows), own_rows)
    for h in range(q_cols // head_dim):
        cols = pl.ds(h * head_dim, head_dim)
        q_out[:, pl.ds(pl.multiple_of(y_idx * q_cols + h * head_dim, head_dim), head_dim)] = rotate(q_bf[own_span, cols])
    y_copy.wait_recv()
    for h in range(q_cols // head_dim):
        cols = pl.ds(h * head_dim, head_dim)
        q_out[:, pl.ds(pl.multiple_of((1 - y_idx) * q_cols + h * head_dim, head_dim), head_dim)] = rotate(q_peer[:, cols])

    for pair in gu_outs:
        for item in pair:
            item.wait()
    for item in [hid_copy, gain_copy, q_copy, kv_copy, y_copy] + remote + remote_gu:
        item.wait_send()
    for step in range(1, x_size):
        stat_copy(step).wait_send()


def project_call(mesh, hidden, gain, cos_a, sin_a, w_query, w_key, w_value, w_gate, w_up):
    y_size, x_size = mesh.shape["yax"], mesh.shape["xax"]
    rows, part = hidden.shape
    own_rows = cos_a.shape[0]
    q_cols = w_query.shape[1]
    head_dim = w_key.shape[1]
    ff_cols = w_gate.shape[1] // x_size
    half = rows // 2
    dma, vm, f32, bf16 = pltpu.SemaphoreType.DMA, pltpu.VMEM, jnp.float32, jnp.bfloat16
    any_spec = pl.BlockSpec(memory_space=pl.ANY)
    vmem_spec = pl.BlockSpec(memory_space=pltpu.VMEM)
    shape = jax.ShapeDtypeStruct
    return pl.pallas_call(
        functools.partial(project_kernel, y_size, x_size),
        out_shape=(shape((own_rows, y_size * q_cols), bf16), shape((own_rows, head_dim), bf16),
                   shape((own_rows, head_dim), bf16), shape((rows, 2 * ff_cols), f32),
                   shape((half, 2 * ff_cols), f32), shape((half, 2 * ff_cols), f32)),
        in_specs=[vmem_spec] * 4 + [any_spec] * 5,
        out_specs=(vmem_spec,) * 3 + (any_spec,) * 3,
        scratch_shapes=[
            vm((rows, part), bf16), vm((8, part), f32), vm((2, part, q_cols), bf16), vm((2, part, 2 * head_dim), bf16),
            vm((2, 2, part, 2 * ff_cols), bf16),
            vm((2, rows, part), bf16), vm((8, rows), f32), vm((x_size, 8, rows), f32),
            vm((2 * own_rows, q_cols), f32), vm((2 * own_rows, q_cols), f32),
            vm((own_rows, 2 * head_dim), f32), vm((own_rows, 2 * head_dim), f32),
            vm((2 * own_rows, q_cols), bf16), vm((own_rows, q_cols), bf16),
            vm((2, 2, half, 2 * ff_cols), f32),
            dma((4,)), dma((x_size,)), dma((x_size,)), dma((7,)), dma((7,)), dma((7,)), dma((4,)), dma((2,)), dma((4,))],
        compiler_params=pltpu.CompilerParams(collective_id=1, has_side_effects=True, vmem_limit_bytes=40 * 1024 * 1024),
        cost_estimate=pl.CostEstimate(flops=2 * rows * part * 2 * (q_cols + 4 * ff_cols), bytes_accessed=30_000_000,
                                      transcendentals=0),
        name="project",
    )(hidden, jnp.broadcast_to(gain[None, :], (8, part)), cos_a, sin_a, w_query, w_key, w_value, w_gate, w_up)


S_CHUNK = 2048
SLOTS = 4


def attend_kernel(len_ref, q_ref, kn_ref, vn_ref, k_hbm, v_hbm, o_ref, k_buf, v_buf, s_buf, sem):
    n_seq, heads, head_dim = q_ref.shape
    scale = head_dim ** -0.5

    def n_chunks(b):
        return (len_ref[b] + (S_CHUNK - 1)) // S_CHUNK

    def copies(b, c, slot):
        span = pl.ds(pl.multiple_of(c * S_CHUNK, S_CHUNK), S_CHUNK)
        return (pltpu.make_async_copy(k_hbm.at[b, span, :], k_buf.at[slot], sem.at[0, slot]),
                pltpu.make_async_copy(v_hbm.at[b, span, :], v_buf.at[slot], sem.at[1, slot]))

    def advance(b, c):
        last = c + 1 >= n_chunks(jnp.minimum(b, n_seq - 1))
        return jnp.where(last, b + 1, b), jnp.where(last, 0, c + 1)

    def fetch(b, c, slot):
        @pl.when(b < n_seq)
        def _():
            for item in copies(b, c, slot):
                item.start()

    total = lax.fori_loop(0, n_seq, lambda b, acc: acc + n_chunks(b), 0)
    ahead = (0, 0)
    for i in range(SLOTS - 1):
        fetch(ahead[0], ahead[1], i)
        ahead = advance(*ahead)

    def scores(b, c, slot):
        raw = lax.dot_general(q_ref[b], k_buf[slot], NT_DIMS, preferred_element_type=jnp.float32) * scale
        pos = lax.broadcasted_iota(jnp.int32, (1, S_CHUNK), 1) + c * S_CHUNK
        return jnp.where(pos < len_ref[b], raw, -1e30)

    def fold(b, c, slot, s_val, state):
        run_max, run_sum, acc = state
        first = c == 0
        fresh = jnp.sum(q_ref[b].astype(jnp.float32) * kn_ref[b].astype(jnp.float32), axis=1, keepdims=True) * scale
        run_max = jnp.where(first, jnp.broadcast_to(fresh, run_max.shape), run_max)
        lane = lax.broadcasted_iota(jnp.int32, run_sum.shape, 1)
        run_sum = jnp.where(first, jnp.where(lane == 0, 1.0, 0.0), run_sum)
        acc = jnp.where(first, jnp.broadcast_to(vn_ref[b].astype(jnp.float32), acc.shape), acc)
        new_max = jnp.maximum(run_max, jnp.max(s_val, axis=1, keepdims=True))
        alpha = jnp.exp(run_max - new_max)
        prob = jnp.exp(s_val - new_max[:, 0:1])
        lanes = prob[:, 0:128]
        for g in range(1, S_CHUNK // 128):
            lanes = lanes + prob[:, g * 128:(g + 1) * 128]
        run_sum = run_sum * alpha + lanes
        acc = acc * alpha + jnp.dot(prob.astype(jnp.bfloat16), v_buf[slot], preferred_element_type=jnp.float32)

        @pl.when(c + 1 >= n_chunks(b))
        def _():
            o_ref[b] = (acc / jnp.sum(run_sum, axis=1, keepdims=True)).astype(jnp.bfloat16)
        return new_max, run_sum, acc

    for item in copies(0, 0, 0):
        item.wait()
    s_buf[...] = scores(0, 0, 0)
    zero = jnp.zeros((heads, 128), jnp.float32)

    def step(i, carry):
        b_prev, c_prev, b_next, c_next, b_ahead, c_ahead, state = carry
        slot_prev = lax.rem(i - 1, SLOTS)
        slot = lax.rem(i, SLOTS)
        fetch(b_ahead, c_ahead, lax.rem(i + SLOTS - 2, SLOTS))
        for item in copies(b_next, c_next, slot):
            item.wait()
        s_prev = s_buf[...]
        s_new = scores(b_next, c_next, slot)
        state = fold(b_prev, c_prev, slot_prev, s_prev, state)
        s_buf[...] = s_new
        return (b_next, c_next, *advance(b_next, c_next), *advance(b_ahead, c_ahead), state)

    b_one, c_one = advance(0, 0)
    carry = lax.fori_loop(1, total, step, (0, 0, b_one, c_one, ahead[0], ahead[1], (zero, zero, zero)))
    fold(carry[0], carry[1], lax.rem(total - 1, SLOTS), s_buf[...], carry[6])


def attend_call(query, k_cache, v_cache, key_new, value_new, lengths):
    n_seq, heads, head_dim = query.shape
    any_spec = pl.BlockSpec(memory_space=pl.ANY)
    vmem_spec = pl.BlockSpec(memory_space=pltpu.VMEM)
    return pl.pallas_call(
        attend_kernel,
        out_shape=jax.ShapeDtypeStruct(query.shape, jnp.bfloat16),
        in_specs=[pl.BlockSpec(memory_space=pltpu.SMEM), vmem_spec, vmem_spec, vmem_spec, any_spec, any_spec],
        out_specs=vmem_spec,
        scratch_shapes=[pltpu.VMEM((SLOTS, S_CHUNK, head_dim), jnp.bfloat16),
                        pltpu.VMEM((SLOTS, S_CHUNK, head_dim), jnp.bfloat16),
                        pltpu.VMEM((heads, S_CHUNK), jnp.float32), pltpu.SemaphoreType.DMA((2, SLOTS))],
        compiler_params=pltpu.CompilerParams(vmem_limit_bytes=32 * 1024 * 1024),
        cost_estimate=pl.CostEstimate(flops=40_000_000_000, bytes_accessed=130_000_000, transcendentals=4_000_000),
        name="attend",
    )(lengths, query, key_new[:, None, :], value_new[:, None, :], k_cache, v_cache)


def head_kernel(y_size, x_size, att_ref, hid_ref, gain_ref, keep_ref, got_a_ref, send_b_ref, w_out_ref, w_down_ref,
                emb_ref, z_ref, norm_ref, ebuf, f_own, f_peer, send, recv, o_all, m_all, w_out, w_down, gu_keep, gu_got,
                sum_own, sum_peer, mom_own, mom_all, stat_own, stat_all,
                own_sem, peer_ssem, peer_rsem, f_ssem, f_rsem, z_ssem, z_rsem, stat_ssem, stat_rsem, out_sem,
                o_ssem, o_rsem, m_ssem, m_rsem, in_sem, gu_sem, sum_ssem, sum_rsem, mom_ssem, mom_rsem):
    y_idx, d_idx, core, chip = positions(x_size)
    partner = 2 * chip + (1 - core)
    x_nbr = 2 * (1 - chip) + core
    x_diag = 2 * (1 - chip) + (1 - core)
    n_dev = y_size * x_size
    flat = y_idx * x_size + d_idx
    v_quarter = recv.shape[1]
    half = recv.shape[2]
    chunks = recv.shape[0]
    full_tiles = v_quarter // V_TILE
    tail = v_quarter - full_tiles * V_TILE
    own_rows = att_ref.shape[0]
    o_cols = o_all.shape[1]
    ff_cols = m_all.shape[3]
    part = hid_ref.shape[1]

    def e_own_copy(quarter, tile, size):
        place = x_nbr if quarter == 0 else d_idx
        start = pl.multiple_of(place * v_quarter + tile * V_TILE, 16)
        off = pl.multiple_of(tile * V_TILE, V_TILE)
        return pltpu.make_async_copy(emb_ref.at[pl.ds(start, size), :], ebuf.at[0, quarter, pl.ds(off, size), :],
                                     own_sem.at[quarter, tile])

    def e_peer_copy(quarter, tile, size):
        place = x_diag if quarter == 0 else partner
        start = pl.multiple_of(place * v_quarter + tile * V_TILE, 16)
        off = pl.multiple_of(tile * V_TILE, V_TILE)
        return pltpu.make_async_remote_copy(
            src_ref=emb_ref.at[pl.ds(start, size), :], dst_ref=ebuf.at[1, quarter, pl.ds(off, size), :],
            send_sem=peer_ssem.at[quarter, tile], recv_sem=peer_rsem.at[quarter, tile],
            device_id={"xax": partner}, device_id_type=MESH)

    def z_copy(chunk, tile, size):
        off = pl.multiple_of(tile * V_TILE, V_TILE)
        return pltpu.make_async_remote_copy(
            src_ref=send.at[chunk, pl.ds(off, size), :], dst_ref=recv.at[chunk, pl.ds(off, size), :],
            send_sem=z_ssem.at[chunk, tile], recv_sem=z_rsem.at[chunk, tile],
            device_id={"xax": x_nbr}, device_id_type=MESH)

    def to_xax(src, dst, ssem, rsem, place):
        return pltpu.make_async_remote_copy(src_ref=src, dst_ref=dst, send_sem=ssem, recv_sem=rsem,
                                            device_id={"xax": place}, device_id_type=MESH)

    def f_copy(chunk):
        return to_xax(f_own.at[chunk], f_peer.at[chunk], f_ssem.at[chunk], f_rsem.at[chunk], partner)

    def m_copy(chunk, which):
        slot, place = ((d_idx, partner), (d_idx, x_nbr), (x_nbr, partner))[which]
        return to_xax(m_all.at[chunk, slot], m_all.at[chunk, slot], m_ssem.at[chunk, which], m_rsem.at[chunk, which],
                      place)

    def sum_copy(chunk):
        return pltpu.make_async_remote_copy(
            src_ref=sum_own.at[chunk], dst_ref=sum_peer.at[chunk], send_sem=sum_ssem.at[chunk],
            recv_sem=sum_rsem.at[chunk], device_id={"yax": 1 - y_idx}, device_id_type=MESH)

    def mom_copy(chunk, step):
        return to_xax(mom_own.at[chunk], mom_all.at[chunk, d_idx], mom_ssem.at[chunk, step], mom_rsem.at[chunk, step],
                      lax.rem(d_idx + step, x_size))

    def o_copy(step):
        other = lax.rem(flat + step, n_dev)
        y_to = other // x_size
        return pltpu.make_async_remote_copy(
            src_ref=att_ref.at[:, pl.ds(pl.multiple_of(y_to * o_cols, 128), o_cols)],
            dst_ref=o_all.at[pl.ds(pl.multiple_of(flat * own_rows, own_rows), own_rows), :],
            send_sem=o_ssem.at[step], recv_sem=o_rsem.at[step],
            device_id={"yax": y_to, "xax": lax.rem(other, x_size)}, device_id_type=MESH)

    def over_tiles(body, low=0, high=None):
        high = full_tiles + 1 if high is None else high

        @pl.loop(low, min(high, full_tiles))
        def _(tile):
            body(tile, V_TILE)
        if high > full_tiles:
            body(full_tiles, tail)

    gu_copy = to_xax(send_b_ref, gu_got.at[1], gu_sem.at[0], gu_sem.at[1], x_nbr)
    ins = [pltpu.make_async_copy(keep_ref.at[pl.ds(0, half), :], gu_keep.at[0], in_sem.at[0]),
           pltpu.make_async_copy(got_a_ref, gu_got.at[0], in_sem.at[1]),
           pltpu.make_async_copy(w_out_ref, w_out, in_sem.at[2]),
           pltpu.make_async_copy(w_down_ref, w_down, in_sem.at[3]),
           pltpu.make_async_copy(keep_ref.at[pl.ds(half, half), :], gu_keep.at[1], in_sem.at[4])]
    for item in ins:
        item.start()
    all_barrier(y_size, x_size, y_idx, d_idx)

    def front_m(chunk):
        gated = gu_keep[chunk] + gu_got[chunk]
        gate = gated[:, :ff_cols].astype(jnp.bfloat16).astype(jnp.float32)
        up_val = gated[:, ff_cols:].astype(jnp.bfloat16).astype(jnp.float32)
        m_all[chunk, d_idx] = (gate * (1.0 / (1.0 + jnp.exp(-gate))) * up_val).astype(jnp.bfloat16)
        m_copy(chunk, 1).start()
        m_copy(chunk, 0).start()

    def front_rest(chunk):
        span = pl.ds(chunk * half, half)

        def down(slot):
            return jnp.dot(m_all[chunk, slot], w_down[pl.ds(pl.multiple_of(slot * ff_cols, ff_cols), ff_cols), :],
                           preferred_element_type=jnp.float32)
        sum_own[chunk] = jnp.dot(o_all[span, :], w_out[...], preferred_element_type=jnp.float32) + down(d_idx)
        m_copy(chunk, 0).wait_recv()
        sum_own[chunk] += down(partner)
        m_copy(chunk, 1).wait_recv()
        m_copy(chunk, 2).start()
        sum_own[chunk] += down(x_nbr)
        m_copy(chunk, 2).wait_recv()
        sum_own[chunk] += down(x_diag)
        sum_copy(chunk).start()
        sum_copy(chunk).wait_recv()
        res = hid_ref[span, :].astype(jnp.float32) + (sum_own[chunk] + sum_peer[chunk])
        packed = compact_rows(*local_moments(res))
        mom_own[chunk] = packed
        mom_all[chunk, d_idx] = packed
        for step in range(1, x_size):
            mom_copy(chunk, step).start()
        for step in range(1, x_size):
            mom_copy(chunk, step).wait_recv()
        mean, rstd = spread_rows(*join_moments([mom_all[chunk, i] for i in range(x_size)], x_size, part))
        f_own[chunk] = ((res - mean) * rstd * gain_ref[0:1, :]).astype(jnp.bfloat16)
        f_copy(chunk).start()

    def partial(chunk, quarter, tile, size):
        off = pl.multiple_of(tile * V_TILE, V_TILE)
        return (lax.dot_general(ebuf[0, quarter, pl.ds(off, size), :], f_own[chunk], NT_DIMS,
                                preferred_element_type=jnp.float32)
                + lax.dot_general(ebuf[1, quarter, pl.ds(off, size), :], f_peer[chunk], NT_DIMS,
                                  preferred_element_type=jnp.float32))

    def send_tiles(chunk, low, high):
        def one(tile, size):
            if chunk == 0:
                e_own_copy(0, tile, size).wait()
                e_peer_copy(0, tile, size).wait_recv()
            off = pl.multiple_of(tile * V_TILE, V_TILE)
            send[chunk, pl.ds(off, size), :] = partial(chunk, 0, tile, size)

        @pl.loop(low, min(high, full_tiles))
        def _(tile):
            one(tile, V_TILE)

            @pl.when(tile > low)
            def _():
                z_copy(chunk, tile - 1, V_TILE).start()
        if high > full_tiles:
            one(full_tiles, tail)
            z_copy(chunk, full_tiles - 1, V_TILE).start()
            z_copy(chunk, full_tiles, tail).start()
        else:
            z_copy(chunk, high - 1, V_TILE).start()

    def out_copy(chunk, tile, size):
        span = pl.ds(pl.multiple_of(tile * V_TILE, V_TILE), size)
        return pltpu.make_async_copy(recv.at[chunk, span, :], z_ref.at[span, pl.ds(chunk * half, half)],
                                     out_sem.at[chunk, tile])

    def take_tile(chunk, tile, size, carry):
        run_max, run_sum = carry
        off = pl.multiple_of(tile * V_TILE, V_TILE)
        if chunk == 0:
            e_own_copy(1, tile, size).wait()
            e_peer_copy(1, tile, size).wait_recv()
        own = partial(chunk, 1, tile, size)
        z_copy(chunk, tile, size).wait_recv()
        z_val = own + recv[chunk, pl.ds(off, size), :]
        recv[chunk, pl.ds(off, size), :] = z_val
        z_grp = z_val.reshape(size // 8, 8, half)
        new_max = jnp.maximum(run_max, jnp.max(z_grp, axis=0))
        new_sum = run_sum * jnp.exp(run_max - new_max) + jnp.sum(jnp.exp(z_grp - new_max[None]), axis=0)
        out_copy(chunk, tile, size).start()
        return new_max, new_sum

    def stat_copy(chunk, step):
        other = lax.rem(flat + step, n_dev)
        return pltpu.make_async_remote_copy(
            src_ref=stat_own.at[chunk], dst_ref=stat_all.at[chunk, flat], send_sem=stat_ssem.at[chunk, step],
            recv_sem=stat_rsem.at[chunk, step],
            device_id={"yax": other // x_size, "xax": lax.rem(other, x_size)}, device_id_type=MESH)

    def gather_chunk(chunk):
        low = jnp.full((8, half), -jnp.inf, jnp.float32)
        carry = take_tile(chunk, 0, V_TILE, (low, jnp.zeros((8, half), jnp.float32)))
        carry = lax.fori_loop(1, full_tiles, lambda tile, c: take_tile(chunk, tile, V_TILE, c), carry)
        run_max, run_sum = take_tile(chunk, full_tiles, tail, carry)
        top = jnp.max(run_max, axis=0, keepdims=True)
        total = jnp.sum(run_sum * jnp.exp(run_max - top), axis=0, keepdims=True)
        sub = lax.broadcasted_iota(jnp.int32, (8, half), 0)
        both = jnp.where(sub == 0, top, total)
        stat_own[chunk] = both
        stat_all[chunk, flat] = both
        for step in range(1, n_dev):
            stat_copy(chunk, step).start()

    def norm_chunk(chunk):
        for step in range(1, n_dev):
            stat_copy(chunk, step).wait_recv()
        tops = [stat_all[chunk, i, 0:1, :] for i in range(n_dev)]
        top_all = tops[0]
        for item in tops[1:]:
            top_all = jnp.maximum(top_all, item)
        sum_all = jnp.zeros_like(top_all)
        for i in range(n_dev):
            sum_all = sum_all + stat_all[chunk, i, 1:2, :] * jnp.exp(tops[i] - top_all)
        norm_ref[:, pl.ds(chunk * half, half)] = top_all + jnp.log(sum_all)

    ins[0].wait()
    ins[1].wait()
    front_m(0)
    for step in range(1, n_dev):
        o_copy(step).start()
    gu_copy.start()
    over_tiles(lambda tile, size: e_own_copy(0, tile, size).start())
    over_tiles(lambda tile, size: e_peer_copy(0, tile, size).start())
    over_tiles(lambda tile, size: e_own_copy(1, tile, size).start())
    over_tiles(lambda tile, size: e_peer_copy(1, tile, size).start())
    o_all[pl.ds(pl.multiple_of(flat * own_rows, own_rows), own_rows), :] = att_ref[
        :, pl.ds(pl.multiple_of(y_idx * o_cols, 128), o_cols)]
    ins[2].wait()
    ins[3].wait()
    for step in range(1, n_dev):
        o_copy(step).wait_recv()
    front_rest(0)
    f_copy(0).wait_recv()
    split = full_tiles // 2
    send_tiles(0, 0, split)
    ins[4].wait()
    gu_copy.wait_recv()
    front_m(1)
    send_tiles(0, split, full_tiles + 1)
    front_rest(1)
    f_copy(1).wait_recv()
    send_tiles(1, 0, full_tiles + 1)
    for chunk in range(chunks):
        gather_chunk(chunk)
    for chunk in range(chunks):
        norm_chunk(chunk)

    gu_copy.wait_send()
    for step in range(1, n_dev):
        o_copy(step).wait_send()
    for chunk in range(chunks):
        f_copy(chunk).wait_send()
        sum_copy(chunk).wait_send()
        for which in range(3):
            m_copy(chunk, which).wait_send()
        for step in range(1, x_size):
            mom_copy(chunk, step).wait_send()
        for step in range(1, n_dev):
            stat_copy(chunk, step).wait_send()
        over_tiles(lambda tile, size: z_copy(chunk, tile, size).wait_send())
        over_tiles(lambda tile, size: e_peer_copy(chunk, tile, size).wait_send())
        over_tiles(lambda tile, size: out_copy(chunk, tile, size).wait())


def head_call(mesh, attn_own, hidden, gain, keep, got_a, send_b, w_out, w_down, embedding):
    y_size, x_size = mesh.shape["yax"], mesh.shape["xax"]
    rows, part = hidden.shape
    v_quarter = embedding.shape[0] // x_size
    half = rows // 2
    tiles = v_quarter // V_TILE + 1
    n_dev = y_size * x_size
    o_cols = w_out.shape[0]
    ff_cols = w_down.shape[0] // x_size
    dma, vm, f32, bf16 = pltpu.SemaphoreType.DMA, pltpu.VMEM, jnp.float32, jnp.bfloat16
    any_spec = pl.BlockSpec(memory_space=pl.ANY)
    vmem_spec = pl.BlockSpec(memory_space=pltpu.VMEM)
    return pl.pallas_call(
        functools.partial(head_kernel, y_size, x_size),
        out_shape=(jax.ShapeDtypeStruct((v_quarter, rows), f32), jax.ShapeDtypeStruct((1, rows), f32)),
        in_specs=[vmem_spec] * 3 + [any_spec] * 6,
        out_specs=(any_spec, vmem_spec),
        scratch_shapes=[
            vm((2, 2, v_quarter, part), bf16), vm((2, half, part), bf16), vm((2, half, part), bf16),
            vm((2, v_quarter, half), f32), vm((2, v_quarter, half), f32),
            vm((rows, o_cols), bf16), vm((2, x_size, half, ff_cols), bf16), vm(w_out.shape, bf16), vm(w_down.shape, bf16),
            vm((2, half, 2 * ff_cols), f32), vm((2, half, 2 * ff_cols), f32),
            vm((2, half, part), f32), vm((2, half, part), f32),
            vm((2, 8, half), f32), vm((2, x_size, 8, half), f32), vm((2, 8, half), f32), vm((2, n_dev, 8, half), f32),
            dma((2, tiles)), dma((2, tiles)), dma((2, tiles)), dma((2,)), dma((2,)), dma((2, tiles)), dma((2, tiles)),
            dma((2, n_dev)), dma((2, n_dev)), dma((2, tiles)),
            dma((n_dev,)), dma((n_dev,)), dma((2, 3)), dma((2, 3)), dma((5,)), dma((2,)), dma((2,)), dma((2,)),
            dma((2, x_size)), dma((2, x_size))],
        compiler_params=pltpu.CompilerParams(collective_id=0, has_side_effects=True,
                                             vmem_limit_bytes=63 * 1024 * 1024),
        cost_estimate=pl.CostEstimate(flops=2 * rows * 2 * v_quarter * 2 * part, bytes_accessed=40_000_000,
                                      transcendentals=rows * v_quarter),
        name="head",
    )(attn_own, hidden, jnp.broadcast_to(gain[None, :], (8, part)), keep, got_a, send_b, w_out, w_down, embedding)


def solution(mesh):
    y_size = mesh.shape["yax"]
    x_size = mesh.shape["xax"]
    row_spec = P(("dp", "yax", "xax"))

    def local_step(hidden, cache_len, k_cache, v_cache, g_attn, w_query, w_key, w_value,
                   w_gate, w_up, w_out, w_down, g_final, embedding):
        rows = hidden.shape[0]
        own_rows = k_cache.shape[0]
        head_dim = k_cache.shape[2]
        heads = y_size * w_query.shape[1] // head_dim
        own_start = (lax.axis_index("yax") * x_size + lax.axis_index("xax")) * own_rows
        len_own = lax.dynamic_slice_in_dim(cache_len, own_start, own_rows, axis=0)
        angles = rope_angle(len_own, head_dim)
        cos_a, sin_a = jnp.cos(angles), jnp.sin(angles)
        cos_a = jnp.concatenate([cos_a, cos_a], axis=1)
        sin_a = jnp.concatenate([-sin_a, sin_a], axis=1)
        query, key_own, value_own, keep, send_a, send_b = project_call(
            mesh, hidden, g_attn, cos_a, sin_a, w_query, w_key, w_value, w_gate, w_up)
        got_a = lax.ppermute(send_a, "xax", [(i, (i + x_size // 2) % x_size) for i in range(x_size)])
        attn_own = attend_call(query.reshape(own_rows, heads, head_dim), k_cache, v_cache, key_own, value_own, len_own)
        z_val, log_norm = head_call(mesh, attn_own.reshape(own_rows, heads * head_dim), hidden, g_final, keep, got_a,
                                    send_b, w_out, w_down, embedding)
        return key_own, value_own, (z_val - log_norm).T, log_norm.reshape(rows)

    in_specs = (P("dp", "xax"), P("dp"), row_spec, row_spec, P("xax"), P("xax", "yax"),
                P("xax", None), P("xax", None), P("xax", "yax"), P("xax", "yax"),
                P("yax", "xax"), P("yax", "xax"), P("xax"), P("yax", "xax"))
    out_specs = (row_spec, row_spec, P("dp", ("yax", "xax")), P("dp"))
    return jax.shard_map(local_step, mesh=mesh, in_specs=in_specs, out_specs=out_specs, check_vma=False)
```

time: 529 us -> 292 us (0.55)
  blocking collectives: 193 us -> 0 us
  Pallas kernels: 170 us -> 268 us
  matrix products: 83 us -> 0 us
  waiting for transfers between devices: 32 us -> 0.01 us
  between operations: 14.2 us -> 0.75 us
  other arithmetic: 17.9 us -> 6.99 us
  starting transfers between devices: 7.2 us -> 0.92 us
    psum x3 -> x0, blocking collectives: 184 us -> none  [the longest x1 168 us: local_step(): projected = lax.psum(proj_part, 'xax').astype(jnp.bfloat16)]
    dot_general x10 -> x0, matrix products: 83 us -> none  [the longest x1 33 us: attend_local(): jnp.einsum('bhe,bse->bhs', query, k_cache, preferred_element_type=jnp.flo...]
    pallas_call x0 -> x2, Pallas kernels: none -> 68.9 us  [the longest x1 48.4 us: attend_call(): pl.pallas_call(attend_kernel, out_shape=jax.ShapeDtypeStruct(query.shape,...]
    pallas_call x1, Pallas kernels: 170 us -> 199 us  [head_call(): pl.pallas_call(functools.partial(head_kernel, y_size, x_size), out_shape=...]
    psum x1 -> x0, waiting for transfers between devices: 21.8 us -> none  [local_step(): residual_out = residual + lax.psum(branch_sum, 'yax')]
    reduce_sum x3 -> x0, other arithmetic: 10.8 us -> none  [the longest x1 8.41 us: attend_local(): denominator = jnp.sum(weights, axis=-1) + weight_new]
    all_to_all x2 -> x0, waiting for transfers between devices: 10.2 us -> none  [the longest x1 7.62 us: local_step(): query_grp = lax.all_to_all(query, 'yax', 0, 1, tiled=True)]
    all_gather x1 -> x0, blocking collectives: 9.66 us -> none  [local_step(): attn_grp = lax.all_gather(attn_own, 'xax', axis=0, tiled=True)]
  transfers between devices with their start and end apart: 3 -> 1, of which waited for: 3 -> 0; matrix products, arithmetic and copies ran while one was open for 1% -> 0% of each run, Pallas kernels for 0% -> 17%
where the time goes in v2:
time: 292 us; the launch traced here: 290 us
  Pallas kernels  268 us (92%)
  local copies, waits for them, and re-layouts  13.1 us (4%)
  other arithmetic  6.99 us (2%)
    pallas_call x1, Pallas kernels, head_call(): pl.pallas_call(functools.partial(head_kernel, y_size, x_size), out_shape=...  199 us
    pallas_call x1, Pallas kernels, attend_call(): pl.pallas_call(attend_kernel, out_shape=jax.ShapeDtypeStruct(query.shape,...  48.4 us
    pallas_call x1, Pallas kernels, project_call(): pl.pallas_call(functools.partial(project_kernel, y_size, x_size), out_sha...  20.5 us
    unnamed x27, local copies, waits for them, and re-layouts  11.8 us
    transpose x1, other arithmetic, local_step(): return (key_own, value_own, (z_val - log_norm).T, log_norm.reshape(rows))  6 us
  transfers between devices with their start and end apart: 1, of which 0 were waited for; matrix products, arithmetic and copies ran while one was open for 0% of the time, Pallas kernels for 17%

profile of v2, /device:TPU:0, one launch (start us, length us, event | category | flops | bytes accessed | tf_op | source)
XLA Modules:
  0.0 289.9 jit_solution(4405239781419069910)
XLA Ops:
  0.7 0.8 fusion.1
  1.4 0.1 fusion
  1.6 0.1 pad_maximum_fusion
  1.6 0.7 broadcast_in_dim.8.gain_ref
  2.3 0.0 copy-start
  2.3 2.2 copy-done
  4.5 0.0 copy-start.1
  4.5 2.2 copy-done.1
  6.7 0.0 copy-start.3
  6.7 0.9 copy-done.3
  7.7 0.0 copy-start.4
  7.7 1.2 copy-done.4
  8.9 0.0 copy-start.6
  8.9 0.9 copy-done.6
  9.8 0.0 copy-start.7
  9.8 0.9 copy-done.7
  10.7 20.5 %project.1 = (bf16[32,2048]{1,0:T(8,128)(2,1)S(1)}, bf16[32,128]{1,0:T(8,128)(2,1)S(1)}, bf16[32,128]{1,0:T(8,128)(2,1)S(1)}, f32[256,2048]{1,0:T(8,128)S(1)}, f...) custom-call(bf16[256,512]{1,0:T(8,128)(2,1)S(1)} %copy-done.3, f32[8,512]{1,0:T(8,128)S(1)} %broadcast_in_dim.8.gain_ref, ...), custom_call_target="tpu_custom_call" | custom-call | flops 2684354560 | bytes 30000000 | tf_op jit(solution)/shard_map/project/pallas_call | solution.py:244
  31.2 0.0 copy-start.2
  31.2 0.0 copy-start.5
  31.2 0.9 collective-permute-start
  32.2 0.0 copy-start.10
  32.2 48.4 %attend.1 = bf16[32,16,128]{2,1,0:T(8,128)(2,1)S(1)} custom-call(s32[32]{0:T(128)S(1)} %get-tuple-element.21.len_ref, bf16[32,16,128]{2,1,0:T(8,128)(2,1)S(1)} %bitcast.12, bf16[32,1,128]{2,1,0:T(2,128)(2,1)S(1)} %copy.18.kn_ref, bf16[32,1,128]{2,1,0:T(2,128)(2,1)S(1)} %copy.19.vn_ref, bf16[32,8192,128]{2,1,0:T(8,128)(2,1)} %k_hbm.1, ...), custom_call_target="tpu_custom_call" | custom-call | flops 40000000000 | bytes 130000000 | tf_op jit(solution)/shard_map/attend/pallas_call | solution.py:353
  80.6 0.0 copy-done.2
  80.6 0.0 copy-done.5
  80.6 0.7 copy.23
  81.3 0.0 collective-permute-done.got_a_ref
  81.3 0.0 copy-start.8
  81.3 1.0 copy-done.8
  82.3 0.0 copy-done.10
  82.3 0.6 broadcast_in_dim.11.gain_ref
  82.9 199.2 %head.1 = (f32[6288,256]{1,0:T(8,128)}, f32[1,256]{1,0:T(1,128)}) custom-call(bf16[32,2048]{1,0:T(8,128)(2,1)} %bitcast.16, bf16[256,512]{1,0:T(8,128)(2,1)} %hid_ref.3, f32[8,512]{1,0:T(8,128)} %broadcast_in_dim.11.gain_ref, f32[256,2048]{1,0:T(8,128)} %copy-done.2, f32[128,2048]{1,0:T(8,128)} %copy-done.8, f32[128,2048]{1,0:T(8,128)} %copy-done.5, ...), custom_call_target="tpu_custom_call" | custom-call | flops 6593445888 | bytes 40000000 | tf_op jit(solution)/shard_map/head/pallas_call | solution.py:640
  282.1 0.0 copy-start.9
  282.2 6.0 %subtract_bitcast_fusion = f32[256,6288]{0,1:T(8,128)} fusion(f32[6288,256]{1,0:T(8,128)} %get-tuple-element.18, f32[256]{0:T(256)} %bitcast.17), kind=kLoop, calls=%fused_computation | loop fusion | flops 1609728 | bytes 12878848 | tf_op jit(solution)/shard_map/transpose | solution.py:687
  288.2 0.6 copy.27
  288.8 0.6 copy.28
  289.4 0.0 copy-done.9
  289.4 0.6 copy.29
  (4 shorter events, 0.1 us)
Async XLA Ops:
  2.3 2.2 copy-start
  4.5 2.2 copy-start.1
  6.7 0.9 copy-start.3
  7.7 1.2 copy-start.4
  8.9 0.9 copy-start.6
  9.8 0.9 copy-start.7
  31.2 49.5 %copy-start.2 = (f32[256,2048]{1,0:T(8,128)}, f32[256,2048]{1,0:T(8,128)S(1)}, u32[]{:S(2)}) copy-start(f32[256,2048]{1,0:T(8,128)S(1)} %get-tuple-element.15.keep_ref) | copy-start | bytes 6291460
  31.2 49.5 %copy-start.5 = (f32[128,2048]{1,0:T(8,128)}, f32[128,2048]{1,0:T(8,128)S(1)}, u32[]{:S(2)}) copy-start(f32[128,2048]{1,0:T(8,128)S(1)} %get-tuple-element.17.send_b_ref) | copy-start | bytes 3145732
  31.2 50.1 %collective-permute-start = (f32[128,2048]{1,0:T(8,128)S(1)}, f32[128,2048]{1,0:T(8,128)S(1)}, u32[]{:S(2)}, u32[]{:S(2)}) collective-permute-start(f32[128,2048]{1,0:T(8,128)S(1)} %get-tuple-element.16), channel_id=1, source_target_pairs={{0,2},{1,3},{2,0},{3,1},{4,6},{5,7},{6,4},{7,5}} | collective-permute-start | bytes 3145736 | tf_op jit(solution)/shard_map/ppermute | solution.py:683
  32.2 50.1 %copy-start.10 = (f32[512]{0:T(512)S(1)}, f32[512]{0:T(512)}, u32[]{:S(2)}) copy-start(f32[512]{0:T(512)} %param.26) | copy-start | bytes 6148
  81.3 1.0 copy-start.8
  282.1 7.2 %copy-start.9 = (f32[1,256]{1,0:T(1,128)S(1)}, f32[1,256]{1,0:T(1,128)}, u32[]{:S(2)}) copy-start(f32[1,256]{1,0:T(1,128)} %get-tuple-element.19) | copy-start | bytes 3076

commit v3 on v2

--- a/solution.py
+++ b/solution.py
@@ -73,7 +73,7 @@
 
 def project_kernel(y_size, x_size, hid_ref, gain_ref, cos_ref, sin_ref, wq_ref, wk_ref, wv_ref, wg_ref, wu_ref,
                    q_out, k_out, v_out, keep_out, send_a_out, send_b_out,
-                   hid_peer, gain_peer, wq_buf, wkv_buf, wgu_buf, n_buf, stat_own, stat_all,
+                   hid_peer, gain_own, gain_peer, wq_buf, wkv_buf, wgu_buf, n_buf, stat_own, stat_all,
                    q_send, q_recv, kv_send, kv_recv, q_bf, q_peer, gu_buf,
                    hid_sem, stat_ssem, stat_rsem, wl_sem, wp_ssem, wp_rsem, q_sem, y_sem, out_sem):
     y_idx, d_idx, core, chip = positions(x_size)
@@ -111,7 +111,7 @@
                 send_sem=wp_ssem.at[i], recv_sem=wp_rsem.at[i], device_id={"xax": partner}, device_id_type=MESH))
     hid_copy = pltpu.make_async_remote_copy(src_ref=hid_ref, dst_ref=hid_peer, send_sem=hid_sem.at[0],
                                             recv_sem=hid_sem.at[1], device_id={"xax": partner}, device_id_type=MESH)
-    gain_copy = pltpu.make_async_remote_copy(src_ref=gain_ref, dst_ref=gain_peer, send_sem=hid_sem.at[2],
+    gain_copy = pltpu.make_async_remote_copy(src_ref=gain_own, dst_ref=gain_peer, send_sem=hid_sem.at[2],
                                              recv_sem=hid_sem.at[3], device_id={"xax": partner}, device_id_type=MESH)
 
     def stat_copy(step):
@@ -121,6 +121,7 @@
 
     for item in local:
         item.start()
+    gain_own[...] = jnp.broadcast_to(gain_ref[...], gain_own.shape)
     all_barrier(y_size, x_size, y_idx, d_idx)
     hid_copy.start()
     gain_copy.start()
@@ -249,7 +250,7 @@
         in_specs=[vmem_spec] * 4 + [any_spec] * 5,
         out_specs=(vmem_spec,) * 3 + (any_spec,) * 3,
         scratch_shapes=[
-            vm((rows, part), bf16), vm((8, part), f32), vm((2, part, q_cols), bf16), vm((2, part, 2 * head_dim), bf16),
+            vm((rows, part), bf16), vm((8, part), f32), vm((8, part), f32), vm((2, part, q_cols), bf16), vm((2, part, 2 * head_dim), bf16),
             vm((2, 2, part, 2 * ff_cols), bf16),
             vm((2, rows, part), bf16), vm((8, rows), f32), vm((x_size, 8, rows), f32),
             vm((2 * own_rows, q_cols), f32), vm((2 * own_rows, q_cols), f32),
@@ -257,18 +258,19 @@
             vm((2 * own_rows, q_cols), bf16), vm((own_rows, q_cols), bf16),
             vm((2, 2, half, 2 * ff_cols), f32),
             dma((4,)), dma((x_size,)), dma((x_size,)), dma((7,)), dma((7,)), dma((7,)), dma((4,)), dma((2,)), dma((4,))],
-        compiler_params=pltpu.CompilerParams(collective_id=1, has_side_effects=True, vmem_limit_bytes=40 * 1024 * 1024),
+        compiler_params=pltpu.CompilerParams(collective_id=1, has_side_effects=True, vmem_limit_bytes=63 * 1024 * 1024),
         cost_estimate=pl.CostEstimate(flops=2 * rows * part * 2 * (q_cols + 4 * ff_cols), bytes_accessed=30_000_000,
                                       transcendentals=0),
         name="project",
-    )(hidden, jnp.broadcast_to(gain[None, :], (8, part)), cos_a, sin_a, w_query, w_key, w_value, w_gate, w_up)
+    )(hidden, gain[None, :], cos_a, sin_a, w_query, w_key, w_value, w_gate, w_up)
 
 
 S_CHUNK = 2048
 SLOTS = 4
 
 
-def attend_kernel(len_ref, q_ref, kn_ref, vn_ref, k_hbm, v_hbm, o_ref, k_buf, v_buf, s_buf, sem):
+def attend_kernel(len_ref, q_ref, kn_ref, vn_ref, k_hbm, v_hbm, o_ref, k_out, v_out, kn_buf, vn_buf, k_buf, v_buf, s_buf,
+                  sem):
     n_seq, heads, head_dim = q_ref.shape
     scale = head_dim ** -0.5
 
@@ -296,6 +298,11 @@
         fetch(ahead[0], ahead[1], i)
         ahead = advance(*ahead)
 
+    k_out[...] = kn_ref[...]
+    v_out[...] = vn_ref[...]
+    kn_buf[...] = kn_ref[...].astype(jnp.float32)
+    vn_buf[...] = vn_ref[...].astype(jnp.float32)
+
     def scores(b, c, slot):
         raw = lax.dot_general(q_ref[b], k_buf[slot], NT_DIMS, preferred_element_type=jnp.float32) * scale
         pos = lax.broadcasted_iota(jnp.int32, (1, S_CHUNK), 1) + c * S_CHUNK
@@ -304,11 +311,11 @@
     def fold(b, c, slot, s_val, state):
         run_max, run_sum, acc = state
         first = c == 0
-        fresh = jnp.sum(q_ref[b].astype(jnp.float32) * kn_ref[b].astype(jnp.float32), axis=1, keepdims=True) * scale
+        fresh = jnp.sum(q_ref[b].astype(jnp.float32) * kn_buf[pl.ds(b, 1), :], axis=1, keepdims=True) * scale
         run_max = jnp.where(first, jnp.broadcast_to(fresh, run_max.shape), run_max)
         lane = lax.broadcasted_iota(jnp.int32, run_sum.shape, 1)
         run_sum = jnp.where(first, jnp.where(lane == 0, 1.0, 0.0), run_sum)
-        acc = jnp.where(first, jnp.broadcast_to(vn_ref[b].astype(jnp.float32), acc.shape), acc)
+        acc = jnp.where(first, jnp.broadcast_to(vn_buf[pl.ds(b, 1), :], acc.shape), acc)
         new_max = jnp.maximum(run_max, jnp.max(s_val, axis=1, keepdims=True))
         alpha = jnp.exp(run_max - new_max)
         prob = jnp.exp(s_val - new_max[:, 0:1])
@@ -352,23 +359,25 @@
     vmem_spec = pl.BlockSpec(memory_space=pltpu.VMEM)
     return pl.pallas_call(
         attend_kernel,
-        out_shape=jax.ShapeDtypeStruct(query.shape, jnp.bfloat16),
+        out_shape=(jax.ShapeDtypeStruct(query.shape, jnp.bfloat16), jax.ShapeDtypeStruct(key_new.shape, jnp.bfloat16),
+                   jax.ShapeDtypeStruct(key_new.shape, jnp.bfloat16)),
         in_specs=[pl.BlockSpec(memory_space=pltpu.SMEM), vmem_spec, vmem_spec, vmem_spec, any_spec, any_spec],
-        out_specs=vmem_spec,
-        scratch_shapes=[pltpu.VMEM((SLOTS, S_CHUNK, head_dim), jnp.bfloat16),
+        out_specs=(vmem_spec, vmem_spec, vmem_spec),
+        scratch_shapes=[pltpu.VMEM(key_new.shape, jnp.float32), pltpu.VMEM(key_new.shape, jnp.float32),
+                        pltpu.VMEM((SLOTS, S_CHUNK, head_dim), jnp.bfloat16),
                         pltpu.VMEM((SLOTS, S_CHUNK, head_dim), jnp.bfloat16),
                         pltpu.VMEM((heads, S_CHUNK), jnp.float32), pltpu.SemaphoreType.DMA((2, SLOTS))],
-        compiler_params=pltpu.CompilerParams(vmem_limit_bytes=32 * 1024 * 1024),
+        compiler_params=pltpu.CompilerParams(vmem_limit_bytes=63 * 1024 * 1024),
         cost_estimate=pl.CostEstimate(flops=40_000_000_000, bytes_accessed=130_000_000, transcendentals=4_000_000),
         name="attend",
-    )(lengths, query, key_new[:, None, :], value_new[:, None, :], k_cache, v_cache)
-
-
-def head_kernel(y_size, x_size, att_ref, hid_ref, gain_ref, keep_ref, got_a_ref, send_b_ref, w_out_ref, w_down_ref,
+    )(lengths, query, key_new, value_new, k_cache, v_cache)
+
+
+def head_kernel(y_size, x_size, att_ref, hid_ref, gain_ref, keep_ref, got_a_ref, got_b_ref, w_out_ref, w_down_ref,
                 emb_ref, z_ref, norm_ref, ebuf, f_own, f_peer, send, recv, o_all, m_all, w_out, w_down, gu_keep, gu_got,
                 sum_own, sum_peer, mom_own, mom_all, stat_own, stat_all,
                 own_sem, peer_ssem, peer_rsem, f_ssem, f_rsem, z_ssem, z_rsem, stat_ssem, stat_rsem, out_sem,
-                o_ssem, o_rsem, m_ssem, m_rsem, in_sem, gu_sem, sum_ssem, sum_rsem, mom_ssem, mom_rsem):
+                o_ssem, o_rsem, m_ssem, m_rsem, in_sem, sum_ssem, sum_rsem, mom_ssem, mom_rsem):
     y_idx, d_idx, core, chip = positions(x_size)
     partner = 2 * chip + (1 - core)
     x_nbr = 2 * (1 - chip) + core
@@ -447,12 +456,12 @@
         if high > full_tiles:
             body(full_tiles, tail)
 
-    gu_copy = to_xax(send_b_ref, gu_got.at[1], gu_sem.at[0], gu_sem.at[1], x_nbr)
     ins = [pltpu.make_async_copy(keep_ref.at[pl.ds(0, half), :], gu_keep.at[0], in_sem.at[0]),
            pltpu.make_async_copy(got_a_ref, gu_got.at[0], in_sem.at[1]),
            pltpu.make_async_copy(w_out_ref, w_out, in_sem.at[2]),
            pltpu.make_async_copy(w_down_ref, w_down, in_sem.at[3]),
-           pltpu.make_async_copy(keep_ref.at[pl.ds(half, half), :], gu_keep.at[1], in_sem.at[4])]
+           pltpu.make_async_copy(keep_ref.at[pl.ds(half, half), :], gu_keep.at[1], in_sem.at[4]),
+           pltpu.make_async_copy(got_b_ref, gu_got.at[1], in_sem.at[5])]
     for item in ins:
         item.start()
     all_barrier(y_size, x_size, y_idx, d_idx)
@@ -581,7 +590,6 @@
     front_m(0)
     for step in range(1, n_dev):
         o_copy(step).start()
-    gu_copy.start()
     over_tiles(lambda tile, size: e_own_copy(0, tile, size).start())
     over_tiles(lambda tile, size: e_peer_copy(0, tile, size).start())
     over_tiles(lambda tile, size: e_own_copy(1, tile, size).start())
@@ -597,7 +605,7 @@
     split = full_tiles // 2
     send_tiles(0, 0, split)
     ins[4].wait()
-    gu_copy.wait_recv()
+    ins[5].wait()
     front_m(1)
     send_tiles(0, split, full_tiles + 1)
     front_rest(1)
@@ -608,7 +616,6 @@
     for chunk in range(chunks):
         norm_chunk(chunk)
 
-    gu_copy.wait_send()
     for step in range(1, n_dev):
         o_copy(step).wait_send()
     for chunk in range(chunks):
@@ -625,7 +632,7 @@
         over_tiles(lambda tile, size: out_copy(chunk, tile, size).wait())
 
 
-def head_call(mesh, attn_own, hidden, gain, keep, got_a, send_b, w_out, w_down, embedding):
+def head_call(mesh, attn_own, hidden, gain, keep, got_a, got_b, w_out, w_down, embedding):
     y_size, x_size = mesh.shape["yax"], mesh.shape["xax"]
     rows, part = hidden.shape
     v_quarter = embedding.shape[0] // x_size
@@ -651,14 +658,14 @@
             vm((2, 8, half), f32), vm((2, x_size, 8, half), f32), vm((2, 8, half), f32), vm((2, n_dev, 8, half), f32),
             dma((2, tiles)), dma((2, tiles)), dma((2, tiles)), dma((2,)), dma((2,)), dma((2, tiles)), dma((2, tiles)),
             dma((2, n_dev)), dma((2, n_dev)), dma((2, tiles)),
-            dma((n_dev,)), dma((n_dev,)), dma((2, 3)), dma((2, 3)), dma((5,)), dma((2,)), dma((2,)), dma((2,)),
+            dma((n_dev,)), dma((n_dev,)), dma((2, 3)), dma((2, 3)), dma((6,)), dma((2,)), dma((2,)),
             dma((2, x_size)), dma((2, x_size))],
         compiler_params=pltpu.CompilerParams(collective_id=0, has_side_effects=True,
                                              vmem_limit_bytes=63 * 1024 * 1024),
         cost_estimate=pl.CostEstimate(flops=2 * rows * 2 * v_quarter * 2 * part, bytes_accessed=40_000_000,
                                       transcendentals=rows * v_quarter),
         name="head",
-    )(attn_own, hidden, jnp.broadcast_to(gain[None, :], (8, part)), keep, got_a, send_b, w_out, w_down, embedding)
+    )(attn_own, hidden, gain[None, :], keep, got_a, got_b, w_out, w_down, embedding)
 
 
 def solution(mesh):
@@ -680,10 +687,12 @@
         sin_a = jnp.concatenate([-sin_a, sin_a], axis=1)
         query, key_own, value_own, keep, send_a, send_b = project_call(
             mesh, hidden, g_attn, cos_a, sin_a, w_query, w_key, w_value, w_gate, w_up)
-        got_a = lax.ppermute(send_a, "xax", [(i, (i + x_size // 2) % x_size) for i in range(x_size)])
-        attn_own = attend_call(query.reshape(own_rows, heads, head_dim), k_cache, v_cache, key_own, value_own, len_own)
+        across = [(i, (i + x_size // 2) % x_size) for i in range(x_size)]
+        got_a = lax.ppermute(send_a, "xax", across)
+        got_b = lax.ppermute(send_b, "xax", across)
+        attn_own, key_own, value_own = attend_call(query.reshape(own_rows, heads, head_dim), k_cache, v_cache, key_own, value_own, len_own)
         z_val, log_norm = head_call(mesh, attn_own.reshape(own_rows, heads * head_dim), hidden, g_final, keep, got_a,
-                                    send_b, w_out, w_down, embedding)
+                                    got_b, w_out, w_down, embedding)
         return key_own, value_own, (z_val - log_norm).T, log_norm.reshape(rows)
 
     in_specs = (P("dp", "xax"), P("dp"), row_spec, row_spec, P("xax"), P("xax", "yax"),

time: 292 us -> 283 us (0.969)
  local copies, waits for them, and re-layouts: 13.1 us -> 3.74 us
    unnamed x27 -> x5, local copies, waits for them, and re-layouts: 11.8 us -> 3.74 us
    pallas_call x1, Pallas kernels: 199 us -> 196 us  [head_call(): pl.pallas_call(functools.partial(head_kernel, y_size, x_size), out_shape=...]
  transfers between devices with their start and end apart: 1 -> 2, of which waited for: 0 -> 0; matrix products, arithmetic and copies ran while one was open for 0% -> 1% of each run, Pallas kernels for 17% -> 18%
where the time goes in v3:
time: 283 us; the launch traced here: 282 us
  Pallas kernels  267 us (94%)
  other arithmetic  8.11 us (3%)
  local copies, waits for them, and re-layouts  3.74 us (1%)
    pallas_call x1, Pallas kernels, head_call(): pl.pallas_call(functools.partial(head_kernel, y_size, x_size), out_shape=...  196 us
    pallas_call x1, Pallas kernels, attend_call(): pl.pallas_call(attend_kernel, out_shape=(jax.ShapeDtypeStruct(query.shape...  49.4 us
    pallas_call x1, Pallas kernels, project_call(): pl.pallas_call(functools.partial(project_kernel, y_size, x_size), out_sha...  22.1 us
    transpose x1, other arithmetic, local_step(): return (key_own, value_own, (z_val - log_norm).T, log_norm.reshape(rows))  6 us
  transfers between devices with their start and end apart: 2, of which 0 were waited for; matrix products, arithmetic and copies ran while one was open for 1% of the time, Pallas kernels for 18%

profile of v3, /device:TPU:0, one launch (start us, length us, event | category | flops | bytes accessed | tf_op | source)
XLA Modules:
  0.0 281.9 jit_solution(2443856616700257016)
XLA Ops:
  0.7 1.3 fusion.1
  1.9 0.1 fusion
  2.1 0.7 pad_maximum_fusion
  2.8 22.1 %project.1 = (bf16[32,2048]{1,0:T(8,128)(2,1)}, bf16[32,128]{1,0:T(8,128)(2,1)}, bf16[32,128]{1,0:T(8,128)(2,1)}, f32[256,2048]{1,0:T(8,128)}, f32[128,2048]{1,0:T(8,128)}, /*index=5*/f32[128,2048]{1,0:T(8,128)}) custom-call(bf16[256,512]{1,0:T(8,128)(2,1)} %hid_ref.3, f32[1,512]{1,0:T(1,128)} %bitcast.18, f32[32,128]{1,0:T(8,128)} %get-tuple-element.31.cos_ref, ...), custom_call_target="tpu_custom_call" | custom-call | flops 2684354560 | bytes 30000000 | tf_op jit(solution)/shard_map/project/pallas_call | solution.py:245
  24.9 1.5 collective-permute-start
  26.3 0.6 collective-permute-start.1
  26.9 1.6 copy.18
  28.5 49.4 %attend.1 = (bf16[32,16,128]{2,1,0:T(8,128)(2,1)}, bf16[32,128]{1,0:T(8,128)(2,1)}, bf16[32,128]{1,0:T(8,128)(2,1)}) custom-call(s32[32]{0:T(128)} %get-tuple-element.27.len_ref, bf16[32,16,128]{2,1,0:T(8,128)(2,1)} %bitcast.13, bf16[32,128]{1,0:T(8,128)(2,1)} %get-tuple-element.16.kn_ref, bf16[32,128]{1,0:T(8,128)(2,1)} %get-tuple-element.17.vn_ref, ...), custom_call_target="tpu_custom_call" | custom-call | flops 40000000000 | bytes 130000000 | tf_op jit(solution)/shard_map/attend/pallas_call | solution.py:360
  77.9 1.6 copy.21
  79.5 0.0 collective-permute-done.got_a_ref
  79.5 0.0 collective-permute-done.1.got_b_ref
  79.5 195.8 %head.1 = (f32[6288,256]{1,0:T(8,128)}, f32[1,256]{1,0:T(1,128)}) custom-call(bf16[32,2048]{1,0:T(8,128)(2,1)} %bitcast.11, bf16[256,512]{1,0:T(8,128)(2,1)} %hid_ref.3, f32[1,512]{1,0:T(1,128)} %bitcast.17, f32[256,2048]{1,0:T(8,128)} %get-tuple-element.21.keep_ref, f32[128,2048]{1,0:T(8,128)} %collective-permute-done.got_a_ref, ...), custom_call_target="tpu_custom_call" | custom-call | flops 6593445888 | bytes 40000000 | tf_op jit(solution)/shard_map/head/pallas_call | solution.py:647
  275.3 0.0 copy-start
  275.3 6.0 %subtract_bitcast_fusion = f32[256,6288]{0,1:T(8,128)} fusion(f32[6288,256]{1,0:T(8,128)} %get-tuple-element.24, f32[256]{0:T(256)} %bitcast.15), kind=kLoop, calls=%fused_computation | loop fusion | flops 1609728 | bytes 12878848 | tf_op jit(solution)/shard_map/transpose | solution.py:696
  281.3 0.0 copy-done
  281.3 0.6 copy.23
  (1 shorter events, 0.0 us)
Async XLA Ops:
  24.9 54.6 %collective-permute-start = (f32[128,2048]{1,0:T(8,128)}, f32[128,2048]{1,0:T(8,128)}, u32[]{:S(2)}, u32[]{:S(2)}) collective-permute-start(f32[128,2048]{1,0:T(8,128)} %get-tuple-element.22), channel_id=1, source_target_pairs={{0,2},{1,3},{2,0},{3,1},{4,6},{5,7},{6,4},{7,5}} | collective-permute-start | bytes 3145736 | tf_op jit(solution)/shard_map/ppermute | solution.py:691
  26.3 53.1 %collective-permute-start.1 = (f32[128,2048]{1,0:T(8,128)}, f32[128,2048]{1,0:T(8,128)}, u32[]{:S(2)}, u32[]{:S(2)}) collective-permute-start(f32[128,2048]{1,0:T(8,128)} %get-tuple-element.23), channel_id=1, source_target_pairs={{0,2},{1,3},{2,0},{3,1},{4,6},{5,7},{6,4},{7,5}} | collective-permute-start | bytes 3145736 | tf_op jit(solution)/shard_map/ppermute | solution.py:692
  275.3 6.0 %copy-start = (f32[1,256]{1,0:T(1,128)S(1)}, f32[1,256]{1,0:T(1,128)}, u32[]{:S(2)}) copy-start(f32[1,256]{1,0:T(1,128)} %get-tuple-element.25) | copy-start | bytes 3076
